TPU v7x, 128 devices: a whole 4x4x4 slice. The times are simulated.
128 devices in a mesh: row: 4 (over x), col: 4 (over y_lo, core), layer: 8 (over y_hi, z).
Axes of the slice: x: 4, y: 4 (y_hi: 2, y_lo: 2; y = y_hi * 2 + y_lo), z: 4, core: 2. Of those that a mesh axis runs over, the one named last changes fastest.
Arguments:
- left_factor: float32 [6144, 8192], P('row', 'col'), may hold values from -6 to 6
- right_factor: float32 [8192, 6144], P('row', 'col'), may hold values from -0.0625 to 0.0625
Outputs:
- product: float32 [6144, 6144], P(('row', 'layer'), 'col')
All inputs are finite; a program needn't handle non-finite values.
Results may differ from a plain program's by a relative error of at most 0.000073.
Values sent between devices are 32-bit elements; how exact they have to be, the bound alone decides.
No kernel may reach another device: no remote copies, remote signals or barrier semaphores. Data moves between devices by JAX's collectives and lax.ppermute only.
A program may use at most 192 MiB of HBM per device.

v0:
```python
import functools

import jax
import jax.numpy as jnp
from jax import lax
from jax.experimental import pallas as pl
from jax.experimental.pallas import tpu as pltpu
from jax.sharding import PartitionSpec as P


AXES = ("row", "col", "layer")
BLOCK = 256
VMEM = pl.BlockSpec(memory_space=pltpu.VMEM)


def split(value):
    high = value.astype(jnp.bfloat16)
    return high, (value - high.astype(jnp.float32)).astype(jnp.bfloat16)


def prepare_kernel(b_ref, high_ref, low_ref):
    size = b_ref.shape[0]
    at = pl.ds(pl.program_id(0) * size, size)
    high_ref[at, :], low_ref[at, :] = split(b_ref[...])


def prepare(b):
    depth, width = b.shape
    return pl.pallas_call(
        prepare_kernel,
        grid=(depth // BLOCK,),
        in_specs=[pl.BlockSpec((BLOCK, width), lambda i: (i, 0))],
        out_specs=[VMEM, VMEM],
        out_shape=[pltpu.VMEM(b.shape, jnp.bfloat16)] * 2,
        compiler_params=pltpu.CompilerParams(vmem_limit_bytes=16 << 20),
        name="prepare",
    )(pltpu.with_memory_space_constraint(b, pltpu.HBM))


def multiply_kernel(count, *refs):
    pieces, (high_ref, low_ref), outs = refs[:count], refs[count : count + 2], refs[count + 2 :]
    high, low = split(jnp.concatenate([piece[...] for piece in pieces], 0))
    dot = functools.partial(jnp.dot, preferred_element_type=jnp.float32)
    size = pieces[0].shape[0]
    for start in range(0, high_ref.shape[1], BLOCK):
        at = slice(start, start + BLOCK)
        result = dot(high, high_ref[:, at]) + dot(high, low_ref[:, at]) + dot(low, high_ref[:, at])
        for i, out in enumerate(outs):
            out[:, at] = result[i * size : (i + 1) * size]


def multiply(pieces, b_high, b_low):
    pieces = [pltpu.with_memory_space_constraint(v, pltpu.VMEM) for v in pieces]
    (size, depth), width = pieces[0].shape, b_high.shape[1]
    rows = size * len(pieces)
    return pl.pallas_call(
        functools.partial(multiply_kernel, len(pieces)),
        in_specs=[VMEM] * (len(pieces) + 2),
        out_specs=[VMEM] * len(pieces),
        out_shape=[pltpu.VMEM((size, width), jnp.float32)] * len(pieces),
        compiler_params=pltpu.CompilerParams(vmem_limit_bytes=16 << 20),
        cost_estimate=pl.CostEstimate(
            flops=6 * rows * depth * width, bytes_accessed=4 * rows * depth, transcendentals=0
        ),
    )(*pieces, b_high, b_low)


def after(values, anchors):
    return lax.optimization_barrier((tuple(values), tuple(anchors)))[0]


def per_device(left_factor, right_factor):
    rows, cols, layers = (lax.axis_size(name) for name in AXES)
    x, c, l = (lax.axis_index(name) for name in AXES)
    chunk = left_factor.shape[0] // layers
    quarter = chunk // cols

    def send(value, target):
        pairs = []
        for i in range(rows):
            for j in range(cols):
                for k in range(layers):
                    a, b, d = target(i, j, k)
                    pairs.append(((i * cols + j) * layers + k, (a * cols + b) * layers + d))
        return lax.ppermute(value, AXES, pairs)

    def to_row(shift):
        return lambda i, j, k: ((i + shift) % rows, j, k)

    def over_y(i, j, k):
        return i, j ^ 2, k

    def over_core(i, j, k):
        return i, j ^ 1, k

    def take(layer, block):
        start = layer * chunk + block * quarter
        return lax.dynamic_slice_in_dim(left_factor, start, quarter, 0)

    b_high, b_low = prepare(right_factor)
    mul = lambda pieces: multiply(pieces, b_high, b_low)

    spread = [
        take(l, c),
        send(take(l, c ^ 1), over_core),
        send(take(l, c ^ 2), over_y),
        send(take(l ^ 4, c ^ 3), lambda i, j, k: (i, j ^ 3, k ^ 4)),
    ]
    swap_core, swap_y = c % 2 == 1, c // 2 == 1
    swap_core, swap_y, *spread = lax.optimization_barrier((swap_core, swap_y, *spread))
    pick = lambda s: lax.select_n(((x + s) % rows) ^ c, *spread)

    mine2 = send(pick(2), to_row(2))
    mine3 = send(pick(3), to_row(3))
    mine1 = send(pick(1), to_row(1))
    mine0 = pick(0)
    across0 = send(mine0, over_y)
    across2 = send(mine2, over_y)
    near2 = send(mine2, over_core)
    opposite_e = mul([mine2, near2])
    first_up_e = send(opposite_e[0], to_row(1))
    first_down_e = send(opposite_e[1], to_row(-1))

    mine3, mine1 = after((mine3, mine1), opposite_e)
    across3 = send(mine3, over_y)
    near3 = send(mine3, over_core)
    across1 = send(mine1, over_y)
    near1 = send(mine1, over_core)
    both_e = mul([mine3, near3, mine1, near1])
    up_e = jnp.concatenate([both_e[0] + first_up_e, both_e[1]], 0)
    down_e = jnp.concatenate([both_e[2], both_e[3] + first_down_e], 0)
    up_e = send(up_e, to_row(1))
    down_e = send(down_e, to_row(-1))

    (across2,) = after((across2,), both_e)
    far2 = send(across2, over_core)
    opposite_l = mul([across2, far2])
    first_up_l = send(opposite_l[0], to_row(1))
    first_down_l = send(opposite_l[1], to_row(-1))

    across3, across1 = after((across3, across1), opposite_l)
    far3 = send(across3, over_core)
    far1 = send(across1, over_core)
    both_l = mul([across3, far3, across1, far1])
    up_l = jnp.concatenate([both_l[0] + first_up_l, both_l[1]], 0)
    down_l = jnp.concatenate([both_l[2], both_l[3] + first_down_l], 0)

    mine0, across0 = after((mine0, across0), both_l)
    near0 = send(mine0, over_core)
    far0 = send(across0, over_core)
    own = mul([mine0, near0, across0, far0])

    up_l = send(up_l, to_row(1))
    down_l = send(down_l, to_row(-1))

    total_e = jnp.concatenate(own[:2], 0) + up_e + down_e
    total_l = jnp.concatenate(own[2:], 0) + up_l + down_l
    total = jnp.stack([total_e, total_l]).reshape(2, 2, quarter, -1)
    total = jnp.where(swap_core, total[:, ::-1], total)
    total = jnp.where(swap_y, total[::-1], total)
    return total.reshape(chunk, -1)


def solution(mesh):
    placed = (P("row", "col"), P("row", "col"))

    return jax.shard_map(
        per_device,
        mesh=mesh,
        in_specs=placed,
        out_specs=P(("row", "layer"), "col"),
        check_vma=False,
    )
```

profile of v0, /device:TPU:0, one launch (start us, length us, event | category | flops | bytes accessed | tf_op | source)
XLA Modules:
  0.0 118.8 jit_solution(6644711683481430439)
XLA Ops:
  0.0 1.5 %constant_dynamic-slice_fusion = (f32[48,2048]{1,0:T(8,128)S(1)}, f32[48,2048]{1,0:T(8,128)S(1)}, f32[48,2048]{1,0:T(8,128)S(1)}, f32[48,2048]{1,0:T(8,128)S(1)}) fusion(f32[1536,2048]{1,0:T(8,128)} %param.2, s32[]{:T(128)S(6)} %select_n.166, s32[]{:T(128)S(6)} %select_n.164, s32[]{:T(128)S(6)} %select_n.163, s32[]{:T(128)S(6)} %select_n.165), kind=kLoop, calls=%fused_computation.15 | loop fusion | bytes 3145744 | tf_op jit(solution)/shard_map/dynamic_slice | solution.py:98
  1.5 2.6 %collective-permute-start.2 = (f32[48,2048]{1,0:T(8,128)S(1)}, f32[48,2048]{1,0:T(8,128)S(1)}, u32[]{:S(2)}, u32[]{:S(2)}) collective-permute-start(f32[48,2048]{1,0:T(8,128)S(1)} %get-tuple-element.67), channel_id=1, source_target_pairs={{0,28},{1,29},{2,30},{3,31},{4,24},{5,25},{6,26},{7,27},{8,20},{9,... | collective-permute-start | bytes 1179656 | tf_op jit(solution)/shard_map/ppermute | solution.py:85
  4.1 0.7 collective-permute-start
  4.9 8.8 %collective-permute-done.2 = f32[48,2048]{1,0:T(8,128)S(1)} collective-permute-done((f32[48,2048]{1,0:T(8,128)S(1)}, f32[48,2048]{1,0:T(8,128)S(1)}, u32[]{:S(2)}, u32[]{:S(2)}) %collective-permute-start.2) | collective-permute-done | bytes 393248 | tf_op jit(solution)/shard_map/ppermute | solution.py:85
  13.7 2.1 %collective-permute-done.1 = f32[48,2048]{1,0:T(8,128)S(1)} collective-permute-done((f32[48,2048]{1,0:T(8,128)S(1)}, f32[48,2048]{1,0:T(8,128)S(1)}, u32[]{:S(2)}, u32[]{:S(2)}) %collective-permute-start.1) | collective-permute-done | bytes 393248 | tf_op jit(solution)/shard_map/ppermute | solution.py:85
  16.0 3.1 %collective-permute-start.6 = (f32[48,2048]{1,0:T(8,128)S(1)}, f32[48,2048]{1,0:T(8,128)S(1)}, u32[]{:S(2)}, u32[]{:S(2)}) collective-permute-start(f32[48,2048]{1,0:T(8,128)S(1)} %get-tuple-element.72), channel_id=1, source_target_pairs={{0,64},{1,65},{2,66},{3,67},{4,68},{5,69},{6,70},{7,71},{8,72},{9,... | collective-permute-start | bytes 1179656 | tf_op jit(solution)/shard_map/ppermute | solution.py:85
  19.1 8.6 %collective-permute-done.6.refs_0_ = f32[48,2048]{1,0:T(8,128)S(1)} collective-permute-done((f32[48,2048]{1,0:T(8,128)S(1)}, f32[48,2048]{1,0:T(8,128)S(1)}, u32[]{:S(2)}, u32[]{:S(2)}) %collective-permute-start.6) | collective-permute-done | bytes 393248 | tf_op jit(solution)/shard_map/ppermute | solution.py:85
  27.8 1.5 %collective-permute-start.5 = (f32[48,2048]{1,0:T(8,128)S(1)}, f32[48,2048]{1,0:T(8,128)S(1)}, u32[]{:S(2)}, u32[]{:S(2)}) collective-permute-start(f32[48,2048]{1,0:T(8,128)S(1)} %get-tuple-element.73), channel_id=1, source_target_pairs={{0,32},{1,33},{2,34},{3,35},{4,36},{5,37},{6,38},{7,39},{8,40},{9,... | collective-permute-start | bytes 1179656 | tf_op jit(solution)/shard_map/ppermute | solution.py:85
  29.3 1.7 %collective-permute-start.4 = (f32[48,2048]{1,0:T(8,128)S(1)}, f32[48,2048]{1,0:T(8,128)S(1)}, u32[]{:S(2)}, u32[]{:S(2)}) collective-permute-start(f32[48,2048]{1,0:T(8,128)S(1)} %get-tuple-element.74), channel_id=1, source_target_pairs={{0,96},{1,97},{2,98},{3,99},{4,100},{5,101},{6,102},{7,103},{8,104... | collective-permute-start | bytes 1179656 | tf_op jit(solution)/shard_map/ppermute | solution.py:85
  31.0 7.3 %prepare.1 = (bf16[2048,1536]{1,0:T(8,128)(2,1)S(1)}, bf16[2048,1536]{1,0:T(8,128)(2,1)S(1)}) custom-call(f32[2048,1536]{1,0:T(8,128)} %b_ref.1), custom_call_target="tpu_custom_call" | custom-call | tf_op jit(solution)/shard_map/prepare/pallas_call | solution.py:29
  38.4 3.1 %shard_map.28 = (f32[48,1536]{1,0:T(8,128)S(1)}, f32[48,1536]{1,0:T(8,128)S(1)}) custom-call(f32[48,2048]{1,0:T(8,128)S(1)} %collective-permute-done.6.refs_0_, f32[48,2048]{1,0:T(8,128)S(1)} %collective-permute-done.7.refs_1_, bf16[2048,1536]{1,0:T(8,128)(2,1)S(1)} %get-tuple-element.42.refs_2_.refs_4_, bf16[2048,1536]{1,0:T(8,128)(2,1)S(1)} %get-tuple-element.43.refs_3_.refs_5_), custom_call_target="tpu_custom_call" | custom-call | flops 1811939328 | bytes 786432 | tf_op jit(solution)/shard_map/pallas_call | solution.py:56
  41.6 0.5 collective-permute-start.12
  42.5 0.8 collective-permute-done.11.refs_1_
  43.3 0.6 collective-permute-done.12.refs_3_
  43.9 3.8 %shard_map.29 = (f32[48,1536]{1,0:T(8,128)S(1)}, f32[48,1536]{1,0:T(8,128)S(1)}, f32[48,1536]{1,0:T(8,128)S(1)}, f32[48,1536]{1,0:T(8,128)S(1)}) custom-call(f32[48,2048]{1,0:T(8,128)S(1)} %collective-permute-done.4.refs_0_, f32[48,2048]{1,0:T(8,128)S(1)} %collective-permute-done.11.refs_1_, f32[48,2048]{1,0:T(8,128)S(1)} %collective-permute-done.5.refs_2_, ...), custom_call_target="tpu_custom_call" | custom-call | flops 3623878656 | bytes 1572864 | tf_op jit(solution)/shard_map/pallas_call | solution.py:56
  47.7 5.5 %collective-permute-done.10.refs_0_ = f32[48,2048]{1,0:T(8,128)S(1)} collective-permute-done((f32[48,2048]{1,0:T(8,128)S(1)}, f32[48,2048]{1,0:T(8,128)S(1)}, u32[]{:S(2)}, u32[]{:S(2)}) %collective-permute-start.10) | collective-permute-done | bytes 393248 | tf_op jit(solution)/shard_map/ppermute | solution.py:85
  53.5 2.9 %collective-permute-start.20 = (f32[48,1536]{1,0:T(8,128)S(1)}, f32[48,1536]{1,0:T(8,128)S(1)}, u32[]{:S(2)}, u32[]{:S(2)}) collective-permute-start(f32[48,1536]{1,0:T(8,128)S(1)} %get-tuple-element.45), channel_id=1, source_target_pairs={{0,96},{1,97},{2,98},{3,99},{4,100},{5,101},{6,102},{7,103},{8,104... | collective-permute-start | bytes 884744 | tf_op jit(solution)/shard_map/ppermute | solution.py:85
  56.9 1.6 %collective-permute-start.9 = (f32[48,2048]{1,0:T(8,128)S(1)}, f32[48,2048]{1,0:T(8,128)S(1)}, u32[]{:S(2)}, u32[]{:S(2)}) collective-permute-start(f32[48,2048]{1,0:T(8,128)S(1)} %collective-permute-done.5.refs_2_), channel_id=1, source_target_pairs={{0,16},{1,17},{2,18},{3,19},{4,20},{5,21},{6,22},{7,23},{8,24},{9,... | collective-permute-start | bytes 1179656 | tf_op jit(solution)/shard_map/ppermute | solution.py:85
  58.5 5.4 %collective-permute-done.18 = f32[48,1536]{1,0:T(8,128)S(1)} collective-permute-done((f32[48,1536]{1,0:T(8,128)S(1)}, f32[48,1536]{1,0:T(8,128)S(1)}, u32[]{:S(2)}, u32[]{:S(2)}) %collective-permute-start.18) | collective-permute-done | bytes 294944 | tf_op jit(solution)/shard_map/ppermute | solution.py:85
  63.8 0.4 collective-permute-start.3
  64.4 3.1 %shard_map.30 = (f32[48,1536]{1,0:T(8,128)S(1)}, f32[48,1536]{1,0:T(8,128)S(1)}) custom-call(f32[48,2048]{1,0:T(8,128)S(1)} %collective-permute-done.10.refs_0_, f32[48,2048]{1,0:T(8,128)S(1)} %collective-permute-done.13.refs_1_, bf16[2048,1536]{1,0:T(8,128)(2,1)S(1)} %get-tuple-element.42.refs_2_.refs_4_, ...), custom_call_target="tpu_custom_call" | custom-call | flops 1811939328 | bytes 786432 | tf_op jit(solution)/shard_map/pallas_call | solution.py:56
  67.5 0.9 collective-permute-done.8.refs_0_
  68.4 8.4 %collective-permute-done.9.refs_2_ = f32[48,2048]{1,0:T(8,128)S(1)} collective-permute-done((f32[48,2048]{1,0:T(8,128)S(1)}, f32[48,2048]{1,0:T(8,128)S(1)}, u32[]{:S(2)}, u32[]{:S(2)}) %collective-permute-start.9) | collective-permute-done | bytes 393248 | tf_op jit(solution)/shard_map/ppermute | solution.py:85
  76.9 0.5 collective-permute-start.15
  77.5 3.2 %collective-permute-start.21 = (f32[96,1536]{1,0:T(8,128)S(1)}, f32[96,1536]{1,0:T(8,128)S(1)}, u32[]{:S(2)}, u32[]{:S(2)}) collective-permute-start(f32[96,1536]{1,0:T(8,128)S(1)} %pad_maximum_fusion.2), channel_id=1, source_target_pairs={{0,96},{1,97},{2,98},{3,99},{4,100},{5,101},{6,102},{7,103},{8,104... | collective-permute-start | bytes 1769480 | tf_op jit(solution)/shard_map/ppermute | solution.py:85
  80.8 3.2 %collective-permute-start.24 = (f32[48,1536]{1,0:T(8,128)S(1)}, f32[48,1536]{1,0:T(8,128)S(1)}, u32[]{:S(2)}, u32[]{:S(2)}) collective-permute-start(f32[48,1536]{1,0:T(8,128)S(1)} %get-tuple-element.54), channel_id=1, source_target_pairs={{0,96},{1,97},{2,98},{3,99},{4,100},{5,101},{6,102},{7,103},{8,104... | collective-permute-start | bytes 884744 | tf_op jit(solution)/shard_map/ppermute | solution.py:85
  84.0 3.8 %shard_map.31 = (f32[48,1536]{1,0:T(8,128)S(1)}, f32[48,1536]{1,0:T(8,128)S(1)}, f32[48,1536]{1,0:T(8,128)S(1)}, f32[48,1536]{1,0:T(8,128)S(1)}) custom-call(f32[48,2048]{1,0:T(8,128)S(1)} %collective-permute-done.8.refs_0_, f32[48,2048]{1,0:T(8,128)S(1)} %collective-permute-done.14.refs_1_, f32[48,2048]{1,0:T(8,128)S(1)} %collective-permute-done.9.refs_2_, ...), custom_call_target="tpu_custom_call" | custom-call | flops 3623878656 | bytes 1572864 | tf_op jit(solution)/shard_map/pallas_call | solution.py:56
  87.9 12.4 %collective-permute-done.22 = f32[48,1536]{1,0:T(8,128)S(1)} collective-permute-done((f32[48,1536]{1,0:T(8,128)S(1)}, f32[48,1536]{1,0:T(8,128)S(1)}, u32[]{:S(2)}, u32[]{:S(2)}) %collective-permute-start.22) | collective-permute-done | bytes 294944 | tf_op jit(solution)/shard_map/ppermute | solution.py:85
  100.6 3.3 %collective-permute-start.25 = (f32[96,1536]{1,0:T(8,128)S(1)}, f32[96,1536]{1,0:T(8,128)S(1)}, u32[]{:S(2)}, u32[]{:S(2)}) collective-permute-start(f32[96,1536]{1,0:T(8,128)S(1)} %pad_maximum_fusion.4), channel_id=1, source_target_pairs={{0,96},{1,97},{2,98},{3,99},{4,100},{5,101},{6,102},{7,103},{8,104... | collective-permute-start | bytes 1769480 | tf_op jit(solution)/shard_map/ppermute | solution.py:85
  103.9 3.8 %shard_map.32 = (f32[48,1536]{1,0:T(8,128)S(1)}, f32[48,1536]{1,0:T(8,128)S(1)}, f32[48,1536]{1,0:T(8,128)S(1)}, f32[48,1536]{1,0:T(8,128)S(1)}) custom-call(f32[48,2048]{1,0:T(8,128)S(1)} %get-tuple-element.61.refs_0_, f32[48,2048]{1,0:T(8,128)S(1)} %collective-permute-done.16.refs_1_, f32[48,2048]{1,0:T(8,128)S(1)} %collective-permute-done.3.refs_2_, ...), custom_call_target="tpu_custom_call" | custom-call | flops 3623878656 | bytes 1572864 | tf_op jit(solution)/shard_map/pallas_call | solution.py:56
  107.8 9.6 %collective-permute-done.23 = f32[96,1536]{1,0:T(8,128)S(1)} collective-permute-done((f32[96,1536]{1,0:T(8,128)S(1)}, f32[96,1536]{1,0:T(8,128)S(1)}, u32[]{:S(2)}, u32[]{:S(2)}) %collective-permute-start.23) | collective-permute-done | bytes 589856 | tf_op jit(solution)/shard_map/ppermute | solution.py:85
  117.7 1.1 reverse_select_fusion
  (41 shorter events, 2.6 us)
Async XLA Ops:
  1.5 12.2 %collective-permute-start.2 = (f32[48,2048]{1,0:T(8,128)S(1)}, f32[48,2048]{1,0:T(8,128)S(1)}, u32[]{:S(2)}, u32[]{:S(2)}) collective-permute-start(f32[48,2048]{1,0:T(8,128)S(1)} %get-tuple-element.67), channel_id=1, source_target_pairs={{0,28},{1,29},{2,30},{3,31},{4,24},{5,25},{6,26},{7,27},{8,20},{9,... | collective-permute-start | bytes 1179656 | tf_op jit(solution)/shard_map/ppermute | solution.py:85
  4.1 9.6 %collective-permute-start = (f32[48,2048]{1,0:T(8,128)S(1)}, f32[48,2048]{1,0:T(8,128)S(1)}, u32[]{:S(2)}, u32[]{:S(2)}) collective-permute-start(f32[48,2048]{1,0:T(8,128)S(1)} %get-tuple-element.68), channel_id=1, source_target_pairs={{0,8},{1,9},{2,10},{3,11},{4,12},{5,13},{6,14},{7,15},{8,0},{9,1},... | collective-permute-start | bytes 1179656 | tf_op jit(solution)/shard_map/ppermute | solution.py:85
  4.8 11.0 %collective-permute-start.1 = (f32[48,2048]{1,0:T(8,128)S(1)}, f32[48,2048]{1,0:T(8,128)S(1)}, u32[]{:S(2)}, u32[]{:S(2)}) collective-permute-start(f32[48,2048]{1,0:T(8,128)S(1)} %get-tuple-element.70), channel_id=1, source_target_pairs={{0,16},{1,17},{2,18},{3,19},{4,20},{5,21},{6,22},{7,23},{8,24},{9,... | collective-permute-start | bytes 1179656 | tf_op jit(solution)/shard_map/ppermute | solution.py:85
  16.0 11.7 %collective-permute-start.6 = (f32[48,2048]{1,0:T(8,128)S(1)}, f32[48,2048]{1,0:T(8,128)S(1)}, u32[]{:S(2)}, u32[]{:S(2)}) collective-permute-start(f32[48,2048]{1,0:T(8,128)S(1)} %get-tuple-element.72), channel_id=1, source_target_pairs={{0,64},{1,65},{2,66},{3,67},{4,68},{5,69},{6,70},{7,71},{8,72},{9,... | collective-permute-start | bytes 1179656 | tf_op jit(solution)/shard_map/ppermute | solution.py:85
  27.8 10.6 %collective-permute-start.7 = (f32[48,2048]{1,0:T(8,128)S(1)}, f32[48,2048]{1,0:T(8,128)S(1)}, u32[]{:S(2)}, u32[]{:S(2)}) collective-permute-start(f32[48,2048]{1,0:T(8,128)S(1)} %collective-permute-done.6.refs_0_), channel_id=1, source_target_pairs={{0,8},{1,9},{2,10},{3,11},{4,12},{5,13},{6,14},{7,15},{8,0},{9,1},... | collective-permute-start | bytes 1179656 | tf_op jit(solution)/shard_map/ppermute | solution.py:85
  27.8 13.7 %collective-permute-start.5 = (f32[48,2048]{1,0:T(8,128)S(1)}, f32[48,2048]{1,0:T(8,128)S(1)}, u32[]{:S(2)}, u32[]{:S(2)}) collective-permute-start(f32[48,2048]{1,0:T(8,128)S(1)} %get-tuple-element.73), channel_id=1, source_target_pairs={{0,32},{1,33},{2,34},{3,35},{4,36},{5,37},{6,38},{7,39},{8,40},{9,... | collective-permute-start | bytes 1179656 | tf_op jit(solution)/shard_map/ppermute | solution.py:85
  29.3 12.2 %collective-permute-start.4 = (f32[48,2048]{1,0:T(8,128)S(1)}, f32[48,2048]{1,0:T(8,128)S(1)}, u32[]{:S(2)}, u32[]{:S(2)}) collective-permute-start(f32[48,2048]{1,0:T(8,128)S(1)} %get-tuple-element.74), channel_id=1, source_target_pairs={{0,96},{1,97},{2,98},{3,99},{4,100},{5,101},{6,102},{7,103},{8,104... | collective-permute-start | bytes 1179656 | tf_op jit(solution)/shard_map/ppermute | solution.py:85
  41.5 1.8 %collective-permute-start.11 = (f32[48,2048]{1,0:T(8,128)S(1)}, f32[48,2048]{1,0:T(8,128)S(1)}, u32[]{:S(2)}, u32[]{:S(2)}) collective-permute-start(f32[48,2048]{1,0:T(8,128)S(1)} %collective-permute-done.4.refs_0_), channel_id=1, source_target_pairs={{0,8},{1,9},{2,10},{3,11},{4,12},{5,13},{6,14},{7,15},{8,0},{9,1},... | collective-permute-start | bytes 1179656 | tf_op jit(solution)/shard_map/ppermute | solution.py:85
  41.6 2.3 %collective-permute-start.12 = (f32[48,2048]{1,0:T(8,128)S(1)}, f32[48,2048]{1,0:T(8,128)S(1)}, u32[]{:S(2)}, u32[]{:S(2)}) collective-permute-start(f32[48,2048]{1,0:T(8,128)S(1)} %collective-permute-done.5.refs_2_), channel_id=1, source_target_pairs={{0,8},{1,9},{2,10},{3,11},{4,12},{5,13},{6,14},{7,15},{8,0},{9,1},... | collective-permute-start | bytes 1179656 | tf_op jit(solution)/shard_map/ppermute | solution.py:85
  42.1 11.1 %collective-permute-start.10 = (f32[48,2048]{1,0:T(8,128)S(1)}, f32[48,2048]{1,0:T(8,128)S(1)}, u32[]{:S(2)}, u32[]{:S(2)}) collective-permute-start(f32[48,2048]{1,0:T(8,128)S(1)} %collective-permute-done.6.refs_0_), channel_id=1, source_target_pairs={{0,16},{1,17},{2,18},{3,19},{4,20},{5,21},{6,22},{7,23},{8,24},{9,... | collective-permute-start | bytes 1179656 | tf_op jit(solution)/shard_map/ppermute | solution.py:85
  53.2 11.2 %collective-permute-start.13 = (f32[48,2048]{1,0:T(8,128)S(1)}, f32[48,2048]{1,0:T(8,128)S(1)}, u32[]{:S(2)}, u32[]{:S(2)}) collective-permute-start(f32[48,2048]{1,0:T(8,128)S(1)} %collective-permute-done.10.refs_0_), channel_id=1, source_target_pairs={{0,8},{1,9},{2,10},{3,11},{4,12},{5,13},{6,14},{7,15},{8,0},{9,1},... | collective-permute-start | bytes 1179656 | tf_op jit(solution)/shard_map/ppermute | solution.py:85
  53.2 10.6 %collective-permute-start.18 = (f32[48,1536]{1,0:T(8,128)S(1)}, f32[48,1536]{1,0:T(8,128)S(1)}, u32[]{:S(2)}, u32[]{:S(2)}) collective-permute-start(f32[48,1536]{1,0:T(8,128)S(1)} %get-tuple-element.44), channel_id=1, source_target_pairs={{0,32},{1,33},{2,34},{3,35},{4,36},{5,37},{6,38},{7,39},{8,40},{9,... | collective-permute-start | bytes 884744 | tf_op jit(solution)/shard_map/ppermute | solution.py:85
  53.5 10.8 %collective-permute-start.20 = (f32[48,1536]{1,0:T(8,128)S(1)}, f32[48,1536]{1,0:T(8,128)S(1)}, u32[]{:S(2)}, u32[]{:S(2)}) collective-permute-start(f32[48,1536]{1,0:T(8,128)S(1)} %get-tuple-element.45), channel_id=1, source_target_pairs={{0,96},{1,97},{2,98},{3,99},{4,100},{5,101},{6,102},{7,103},{8,104... | collective-permute-start | bytes 884744 | tf_op jit(solution)/shard_map/ppermute | solution.py:85
  56.4 12.0 %collective-permute-start.8 = (f32[48,2048]{1,0:T(8,128)S(1)}, f32[48,2048]{1,0:T(8,128)S(1)}, u32[]{:S(2)}, u32[]{:S(2)}) collective-permute-start(f32[48,2048]{1,0:T(8,128)S(1)} %collective-permute-done.4.refs_0_), channel_id=1, source_target_pairs={{0,16},{1,17},{2,18},{3,19},{4,20},{5,21},{6,22},{7,23},{8,24},{9,... | collective-permute-start | bytes 1179656 | tf_op jit(solution)/shard_map/ppermute | solution.py:85
  56.9 20.0 %collective-permute-start.9 = (f32[48,2048]{1,0:T(8,128)S(1)}, f32[48,2048]{1,0:T(8,128)S(1)}, u32[]{:S(2)}, u32[]{:S(2)}) collective-permute-start(f32[48,2048]{1,0:T(8,128)S(1)} %collective-permute-done.5.refs_2_), channel_id=1, source_target_pairs={{0,16},{1,17},{2,18},{3,19},{4,20},{5,21},{6,22},{7,23},{8,24},{9,... | collective-permute-start | bytes 1179656 | tf_op jit(solution)/shard_map/ppermute | solution.py:85
  63.8 24.0 %collective-permute-start.3 = (f32[48,2048]{1,0:T(8,128)S(1)}, f32[48,2048]{1,0:T(8,128)S(1)}, u32[]{:S(2)}, u32[]{:S(2)}) collective-permute-start(f32[48,2048]{1,0:T(8,128)S(1)} %get-tuple-element.61.refs_0_), channel_id=1, source_target_pairs={{0,16},{1,17},{2,18},{3,19},{4,20},{5,21},{6,22},{7,23},{8,24},{9,... | collective-permute-start | bytes 1179656 | tf_op jit(solution)/shard_map/ppermute | solution.py:85
  76.9 3.9 %collective-permute-start.14 = (f32[48,2048]{1,0:T(8,128)S(1)}, f32[48,2048]{1,0:T(8,128)S(1)}, u32[]{:S(2)}, u32[]{:S(2)}) collective-permute-start(f32[48,2048]{1,0:T(8,128)S(1)} %collective-permute-done.8.refs_0_), channel_id=1, source_target_pairs={{0,8},{1,9},{2,10},{3,11},{4,12},{5,13},{6,14},{7,15},{8,0},{9,1},... | collective-permute-start | bytes 1179656 | tf_op jit(solution)/shard_map/ppermute | solution.py:85
  76.9 3.9 %collective-permute-start.15 = (f32[48,2048]{1,0:T(8,128)S(1)}, f32[48,2048]{1,0:T(8,128)S(1)}, u32[]{:S(2)}, u32[]{:S(2)}) collective-permute-start(f32[48,2048]{1,0:T(8,128)S(1)} %collective-permute-done.9.refs_2_), channel_id=1, source_target_pairs={{0,8},{1,9},{2,10},{3,11},{4,12},{5,13},{6,14},{7,15},{8,0},{9,1},... | collective-permute-start | bytes 1179656 | tf_op jit(solution)/shard_map/ppermute | solution.py:85
  77.5 30.2 %collective-permute-start.19 = (f32[96,1536]{1,0:T(8,128)S(1)}, f32[96,1536]{1,0:T(8,128)S(1)}, u32[]{:S(2)}, u32[]{:S(2)}) collective-permute-start(f32[96,1536]{1,0:T(8,128)S(1)} %pad_maximum_fusion.1), channel_id=1, source_target_pairs={{0,32},{1,33},{2,34},{3,35},{4,36},{5,37},{6,38},{7,39},{8,40},{9,... | collective-permute-start | bytes 1769480 | tf_op jit(solution)/shard_map/ppermute | solution.py:85
  77.5 30.2 %collective-permute-start.21 = (f32[96,1536]{1,0:T(8,128)S(1)}, f32[96,1536]{1,0:T(8,128)S(1)}, u32[]{:S(2)}, u32[]{:S(2)}) collective-permute-start(f32[96,1536]{1,0:T(8,128)S(1)} %pad_maximum_fusion.2), channel_id=1, source_target_pairs={{0,96},{1,97},{2,98},{3,99},{4,100},{5,101},{6,102},{7,103},{8,104... | collective-permute-start | bytes 1769480 | tf_op jit(solution)/shard_map/ppermute | solution.py:85
  80.8 19.5 %collective-permute-start.22 = (f32[48,1536]{1,0:T(8,128)S(1)}, f32[48,1536]{1,0:T(8,128)S(1)}, u32[]{:S(2)}, u32[]{:S(2)}) collective-permute-start(f32[48,1536]{1,0:T(8,128)S(1)} %get-tuple-element.53), channel_id=1, source_target_pairs={{0,32},{1,33},{2,34},{3,35},{4,36},{5,37},{6,38},{7,39},{8,40},{9,... | collective-permute-start | bytes 884744 | tf_op jit(solution)/shard_map/ppermute | solution.py:85
  80.8 19.6 %collective-permute-start.24 = (f32[48,1536]{1,0:T(8,128)S(1)}, f32[48,1536]{1,0:T(8,128)S(1)}, u32[]{:S(2)}, u32[]{:S(2)}) collective-permute-start(f32[48,1536]{1,0:T(8,128)S(1)} %get-tuple-element.54), channel_id=1, source_target_pairs={{0,96},{1,97},{2,98},{3,99},{4,100},{5,101},{6,102},{7,103},{8,104... | collective-permute-start | bytes 884744 | tf_op jit(solution)/shard_map/ppermute | solution.py:85
  87.8 12.7 %collective-permute-start.16 = (f32[48,2048]{1,0:T(8,128)S(1)}, f32[48,2048]{1,0:T(8,128)S(1)}, u32[]{:S(2)}, u32[]{:S(2)}) collective-permute-start(f32[48,2048]{1,0:T(8,128)S(1)} %get-tuple-element.61.refs_0_), channel_id=1, source_target_pairs={{0,8},{1,9},{2,10},{3,11},{4,12},{5,13},{6,14},{7,15},{8,0},{9,1},... | collective-permute-start | bytes 1179656 | tf_op jit(solution)/shard_map/ppermute | solution.py:85
  100.3 3.6 %collective-permute-start.17 = (f32[48,2048]{1,0:T(8,128)S(1)}, f32[48,2048]{1,0:T(8,128)S(1)}, u32[]{:S(2)}, u32[]{:S(2)}) collective-permute-start(f32[48,2048]{1,0:T(8,128)S(1)} %collective-permute-done.3.refs_2_), channel_id=1, source_target_pairs={{0,8},{1,9},{2,10},{3,11},{4,12},{5,13},{6,14},{7,15},{8,0},{9,1},... | collective-permute-start | bytes 1179656 | tf_op jit(solution)/shard_map/ppermute | solution.py:85
  100.4 17.0 %collective-permute-start.23 = (f32[96,1536]{1,0:T(8,128)S(1)}, f32[96,1536]{1,0:T(8,128)S(1)}, u32[]{:S(2)}, u32[]{:S(2)}) collective-permute-start(f32[96,1536]{1,0:T(8,128)S(1)} %pad_maximum_fusion.3), channel_id=1, source_target_pairs={{0,32},{1,33},{2,34},{3,35},{4,36},{5,37},{6,38},{7,39},{8,40},{9,... | collective-permute-start | bytes 1769480 | tf_op jit(solution)/shard_map/ppermute | solution.py:85
  100.6 16.8 %collective-permute-start.25 = (f32[96,1536]{1,0:T(8,128)S(1)}, f32[96,1536]{1,0:T(8,128)S(1)}, u32[]{:S(2)}, u32[]{:S(2)}) collective-permute-start(f32[96,1536]{1,0:T(8,128)S(1)} %pad_maximum_fusion.4), channel_id=1, source_target_pairs={{0,96},{1,97},{2,98},{3,99},{4,100},{5,101},{6,102},{7,103},{8,104... | collective-permute-start | bytes 1769480 | tf_op jit(solution)/shard_map/ppermute | solution.py:85
where the time goes:
time: 119 us
  waiting for transfers between devices  63.1 us (53%)
  starting transfers between devices  27 us (23%)
  Pallas kernels  25 us (21%)
  other arithmetic  2.01 us (2%)
  local copies, waits for them, and re-layouts  1.45 us (1%)
    ppermute x26, waiting for transfers between devices, send(): return lax.ppermute(value, AXES, pairs)  63.1 us
    ppermute x26, starting transfers between devices, send(): return lax.ppermute(value, AXES, pairs)  27 us
    pallas_call x5, Pallas kernels, multiply(): pl.pallas_call(functools.partial(multiply_kernel, len(pieces)), in_specs=...  17.7 us
    pallas_call x1, Pallas kernels, prepare(): pl.pallas_call(prepare_kernel, grid=(depth // BLOCK,), in_specs=[pl.Block...  7.33 us
  transfers between devices with their start and end apart: 26, of which 11 were waited for; matrix products, arithmetic and copies ran while one was open for 0% of the time, Pallas kernels for 21%

commit v1 on v0

v1 whole, which is shorter than its diff:
```python
import functools

import jax
import jax.numpy as jnp
from jax import lax
from jax.experimental import pallas as pl
from jax.experimental.pallas import tpu as pltpu
from jax.sharding import PartitionSpec as P


AXES = ("row", "col", "layer")
BLOCK = 256
VMEM = pl.BlockSpec(memory_space=pltpu.VMEM)


def split(value):
    high = value.astype(jnp.bfloat16)
    return high, (value - high.astype(jnp.float32)).astype(jnp.bfloat16)


def prepare_kernel(b_ref, high_ref, low_ref):
    size = b_ref.shape[0]
    at = pl.ds(pl.program_id(0) * size, size)
    high_ref[at, :], low_ref[at, :] = split(b_ref[...])


def prepare(b):
    depth, width = b.shape
    return pl.pallas_call(
        prepare_kernel,
        grid=(depth // BLOCK,),
        in_specs=[pl.BlockSpec((BLOCK, width), lambda i: (i, 0))],
        out_specs=[VMEM, VMEM],
        out_shape=[pltpu.VMEM(b.shape, jnp.bfloat16)] * 2,
        compiler_params=pltpu.CompilerParams(vmem_limit_bytes=16 << 20),
        name="prepare",
    )(pltpu.with_memory_space_constraint(b, pltpu.HBM))


def multiply_kernel(count, *refs):
    pieces, (high_ref, low_ref), outs = refs[:count], refs[count : count + 2], refs[count + 2 :]
    high, low = split(jnp.concatenate([piece[...] for piece in pieces], 0))
    dot = functools.partial(jnp.dot, preferred_element_type=jnp.float32)
    size = outs[0].shape[0]
    for start in range(0, high_ref.shape[1], BLOCK):
        at = slice(start, start + BLOCK)
        result = dot(high, high_ref[:, at]) + dot(high, low_ref[:, at]) + dot(low, high_ref[:, at])
        for i, out in enumerate(outs):
            out[:, at] = result[i * size : (i + 1) * size]


def in_vmem(values):
    return [pltpu.with_memory_space_constraint(v, pltpu.VMEM) for v in values]


def multiply(pieces, b_high, b_low):
    (size, depth), width = pieces[0].shape, b_high.shape[1]
    rows, results = size * len(pieces), len(pieces) // 2
    return pl.pallas_call(
        functools.partial(multiply_kernel, len(pieces)),
        in_specs=[VMEM] * (len(pieces) + 2),
        out_specs=[VMEM] * results,
        out_shape=[pltpu.VMEM((2 * size, width), jnp.float32)] * results,
        compiler_params=pltpu.CompilerParams(vmem_limit_bytes=16 << 20),
        cost_estimate=pl.CostEstimate(
            flops=6 * rows * depth * width, bytes_accessed=4 * rows * depth, transcendentals=0
        ),
    )(*in_vmem(pieces), b_high, b_low)


def choose_kernel(which_ref, *refs):
    for i, value in enumerate(refs[:-1]):

        @pl.when(which_ref[0] == i)
        def _():
            refs[-1][...] = value[...]


def choose(which, values):
    return pl.pallas_call(
        choose_kernel,
        in_specs=[pl.BlockSpec(memory_space=pltpu.SMEM)] + [VMEM] * len(values),
        out_specs=VMEM,
        out_shape=pltpu.VMEM(values[0].shape, values[0].dtype),
        compiler_params=pltpu.CompilerParams(vmem_limit_bytes=4 << 20),
    )(which, *in_vmem(values))


def finish_kernel(col_ref, *refs):
    i, out = pl.program_id(0), refs[-1]
    at = pl.ds(i % 2 * out.shape[0], out.shape[0])
    early, late = refs[:3], refs[3:6]

    @pl.when(i < 2)
    def _():
        out[...] = early[0][at, :] + early[1][at, :] + early[2][at, :]

    @pl.when(i >= 2)
    def _():
        out[...] = late[0][at, :] + late[1][at, :] + late[2][at, :]


def finish(col, early, late):
    rows, width = early[0].shape
    return pl.pallas_call(
        finish_kernel,
        grid_spec=pltpu.PrefetchScalarGridSpec(
            num_scalar_prefetch=1,
            grid=(4,),
            in_specs=[VMEM] * 6,
            out_specs=pl.BlockSpec((rows // 2, width), lambda i, col: (i ^ col[0], 0)),
        ),
        out_shape=jax.ShapeDtypeStruct((2 * rows, width), jnp.float32),
        compiler_params=pltpu.CompilerParams(vmem_limit_bytes=8 << 20),
        name="finish",
    )(col, *in_vmem(early + late))


def after(values, anchors):
    return lax.optimization_barrier((tuple(values), tuple(anchors)))[0]


def per_device(left_factor, right_factor):
    rows, cols, layers = (lax.axis_size(name) for name in AXES)
    x, c, l = (lax.axis_index(name) for name in AXES)
    chunk = left_factor.shape[0] // layers
    quarter = chunk // cols

    def send(value, target):
        pairs = []
        for i in range(rows):
            for j in range(cols):
                for k in range(layers):
                    a, b, d = target(i, j, k)
                    pairs.append(((i * cols + j) * layers + k, (a * cols + b) * layers + d))
        return lax.ppermute(value, AXES, pairs)

    def over_y(i, j, k):
        return i, j ^ 2, k

    def over_core(i, j, k):
        return i, j ^ 1, k

    def take(layer, block):
        start = layer * chunk + block * quarter
        return lax.dynamic_slice_in_dim(left_factor, start, quarter, 0)

    source = lambda s: (((x + s) % rows) ^ c).reshape(1)
    step = jnp.where(c % 2 == 1, 1, rows - 1)
    scalars = (source(2), source(step), source(rows - step), source(0), c.reshape(1))
    taken = (take(l, c), take(l, c ^ 1), take(l, c ^ 2), take(l ^ 4, c ^ 3))
    scalars, taken, right_factor = lax.optimization_barrier((scalars, taken, right_factor))
    source2, source_p, source_q, source0, col = scalars

    b_high, b_low = prepare(right_factor)
    mul = lambda pieces: multiply(pieces, b_high, b_low)

    spread = [
        taken[0],
        send(taken[1], over_core),
        send(taken[2], over_y),
        send(taken[3], lambda i, j, k: (i, j ^ 3, k ^ 4)),
    ]

    def forward(i, j, k):
        return (i + (-1 if j % 2 else 1)) % rows, j, k

    def backward(i, j, k):
        return (i + (1 if j % 2 else -1)) % rows, j, k

    mine2 = send(choose(source2, spread), lambda i, j, k: ((i + 2) % rows, j, k))
    mine_p = send(choose(source_p, spread), backward)
    mine_q = send(choose(source_q, spread), forward)
    mine0 = choose(source0, spread)
    across0 = send(mine0, over_y)
    across2 = send(mine2, over_y)
    near2 = send(mine2, over_core)
    (opposite_e,) = mul([mine2, near2])
    first_e = send(opposite_e, forward)

    mine_p, mine_q, _ = after((mine_p, mine_q, mine2), (opposite_e,))
    across_p = send(mine_p, over_y)
    across_q = send(mine_q, over_y)
    near_p = send(mine_q, over_core)
    near_q = send(mine_p, over_core)
    p_e, q_e = mul([mine_p, near_p, mine_q, near_q])
    from_q_e = send(q_e, backward)
    from_p_e = send(p_e + first_e, forward)

    (across2,) = after((across2,), (p_e,))
    far2 = send(across2, over_core)
    (opposite_l,) = mul([across2, far2])
    first_l = send(opposite_l, forward)

    across_p, across_q = after((across_p, across_q), (opposite_l,))
    far_p = send(across_q, over_core)
    far_q = send(across_p, over_core)
    p_l, q_l = mul([across_p, far_p, across_q, far_q])
    from_q_l = send(q_l, backward)

    mine0, across0 = after((mine0, across0), (p_l,))
    near0 = send(mine0, over_core)
    far0 = send(across0, over_core)
    own_e, own_l = mul([mine0, near0, across0, far0])
    from_p_l = send(p_l + first_l, forward)

    return finish(col, [own_e, from_q_e, from_p_e], [own_l, from_q_l, from_p_l])


def solution(mesh):
    placed = (P("row", "col"), P("row", "col"))

    return jax.shard_map(
        per_device,
        mesh=mesh,
        in_specs=placed,
        out_specs=P(("row", "layer"), "col"),
        check_vma=False,
    )
```

time: 119 us -> 120 us (level)
  waiting for transfers between devices: 63.1 us -> 69.7 us
  starting transfers between devices: 27 us -> 21 us
  other arithmetic: 2.01 us -> 0.14 us
  Pallas kernels: 25 us -> 26.8 us
    ppermute x26 -> x24, waiting for transfers between devices: 63.1 us -> 69.7 us  [send(): return lax.ppermute(value, AXES, pairs)]
    ppermute x26 -> x24, starting transfers between devices: 27 us -> 21 us  [send(): return lax.ppermute(value, AXES, pairs)]
    pallas_call x0 -> x5, Pallas kernels: none -> 1.76 us  [the longest x1 1.62 us: finish(): pl.pallas_call(finish_kernel, grid_spec=pltpu.PrefetchScalarGridSpec(num_...]
    select_n x3 -> x0, other arithmetic: 1.42 us -> none  [the longest x1 1.11 us: per_device(): total = jnp.where(swap_y, total[::-1], total)]
  transfers between devices with their start and end apart: 26 -> 24, of which waited for: 11 -> 14; matrix products, arithmetic and copies ran while one was open for 0% -> 0% of each run, Pallas kernels for 21% -> 21%
where the time goes in v1:
time: 120 us; the launch traced here: 119 us
  waiting for transfers between devices  69.7 us (58%)
  Pallas kernels  26.8 us (22%)
  starting transfers between devices  21 us (18%)
  local copies, waits for them, and re-layouts  1.47 us (1%)
    ppermute x24, waiting for transfers between devices, send(): return lax.ppermute(value, AXES, pairs)  69.7 us
    ppermute x24, starting transfers between devices, send(): return lax.ppermute(value, AXES, pairs)  21 us
    pallas_call x5, Pallas kernels, multiply(): pl.pallas_call(functools.partial(multiply_kernel, len(pieces)), in_specs=...  17.7 us
    pallas_call x1, Pallas kernels, prepare(): pl.pallas_call(prepare_kernel, grid=(depth // BLOCK,), in_specs=[pl.Block...  7.34 us
  transfers between devices with their start and end apart: 24, of which 14 were waited for; matrix products, arithmetic and copies ran while one was open for 0% of the time, Pallas kernels for 21%

profile of v1, /device:TPU:0, one launch (start us, length us, event | category | flops | bytes accessed | tf_op | source)
XLA Modules:
  0.0 119.3 jit_solution(13948085715450047179)
XLA Ops:
  0.0 1.5 %constant_dynamic-slice_fusion = (f32[48,2048]{1,0:T(8,128)S(1)}, f32[48,2048]{1,0:T(8,128)S(1)}, f32[48,2048]{1,0:T(8,128)S(1)}, f32[48,2048]{1,0:T(8,128)S(1)}) fusion(f32[1536,2048]{1,0:T(8,128)} %param.2, s32[]{:T(128)S(6)} %select_n.48, s32[]{:T(128)S(6)} %select_n.46, s32[]{:T(128)S(6)} %select_n.45, s32[]{:T(128)S(6)} %select_n.47), kind=kLoop, calls=%fused_computation | loop fusion | bytes 3145744 | tf_op jit(solution)/shard_map/dynamic_slice | solution.py:146
  1.6 1.8 %collective-permute-start.1 = (f32[48,2048]{1,0:T(8,128)S(1)}, f32[48,2048]{1,0:T(8,128)S(1)}, u32[]{:S(2)}, u32[]{:S(2)}) collective-permute-start(f32[48,2048]{1,0:T(8,128)S(1)} %get-tuple-element.34), channel_id=1, source_target_pairs={{0,16},{1,17},{2,18},{3,19},{4,20},{5,21},{6,22},{7,23},{8,24},{9,... | collective-permute-start | bytes 1179656 | tf_op jit(solution)/shard_map/ppermute | solution.py:136
  3.3 1.9 %collective-permute-start.2 = (f32[48,2048]{1,0:T(8,128)S(1)}, f32[48,2048]{1,0:T(8,128)S(1)}, u32[]{:S(2)}, u32[]{:S(2)}) collective-permute-start(f32[48,2048]{1,0:T(8,128)S(1)} %get-tuple-element.35), channel_id=1, source_target_pairs={{0,28},{1,29},{2,30},{3,31},{4,24},{5,25},{6,26},{7,27},{8,20},{9,... | collective-permute-start | bytes 1179656 | tf_op jit(solution)/shard_map/ppermute | solution.py:136
  5.3 7.8 %collective-permute-done.1.refs_2_ = f32[48,2048]{1,0:T(8,128)S(1)} collective-permute-done((f32[48,2048]{1,0:T(8,128)S(1)}, f32[48,2048]{1,0:T(8,128)S(1)}, u32[]{:S(2)}, u32[]{:S(2)}) %collective-permute-start.1) | collective-permute-done | bytes 393248 | tf_op jit(solution)/shard_map/ppermute | solution.py:136
  13.1 2.6 %collective-permute-done.2.refs_3_ = f32[48,2048]{1,0:T(8,128)S(1)} collective-permute-done((f32[48,2048]{1,0:T(8,128)S(1)}, f32[48,2048]{1,0:T(8,128)S(1)}, u32[]{:S(2)}, u32[]{:S(2)}) %collective-permute-start.2) | collective-permute-done | bytes 393248 | tf_op jit(solution)/shard_map/ppermute | solution.py:136
  15.7 3.1 %collective-permute-start.6 = (f32[48,2048]{1,0:T(8,128)S(1)}, f32[48,2048]{1,0:T(8,128)S(1)}, u32[]{:S(2)}, u32[]{:S(2)}) collective-permute-start(f32[48,2048]{1,0:T(8,128)S(1)} %shard_map.31), channel_id=1, source_target_pairs={{0,64},{1,65},{2,66},{3,67},{4,68},{5,69},{6,70},{7,71},{8,72},{9,... | collective-permute-start | bytes 1179656 | tf_op jit(solution)/shard_map/ppermute | solution.py:136
  18.8 9.6 %collective-permute-done.6.refs_0_ = f32[48,2048]{1,0:T(8,128)S(1)} collective-permute-done((f32[48,2048]{1,0:T(8,128)S(1)}, f32[48,2048]{1,0:T(8,128)S(1)}, u32[]{:S(2)}, u32[]{:S(2)}) %collective-permute-start.6) | collective-permute-done | bytes 393248 | tf_op jit(solution)/shard_map/ppermute | solution.py:136
  28.5 2.9 %collective-permute-start.4 = (f32[48,2048]{1,0:T(8,128)S(1)}, f32[48,2048]{1,0:T(8,128)S(1)}, u32[]{:S(2)}, u32[]{:S(2)}) collective-permute-start(f32[48,2048]{1,0:T(8,128)S(1)} %shard_map.29), channel_id=1, source_target_pairs={{0,96},{1,97},{2,98},{3,99},{4,100},{5,101},{6,102},{7,103},{8,40}... | collective-permute-start | bytes 1179656 | tf_op jit(solution)/shard_map/ppermute | solution.py:136
  31.4 7.3 %prepare.1 = (bf16[2048,1536]{1,0:T(8,128)(2,1)S(1)}, bf16[2048,1536]{1,0:T(8,128)(2,1)S(1)}) custom-call(f32[2048,1536]{1,0:T(8,128)} %b_ref), custom_call_target="tpu_custom_call" | custom-call | tf_op jit(solution)/shard_map/prepare/pallas_call | solution.py:29
  38.8 3.1 %shard_map.32 = f32[96,1536]{1,0:T(8,128)S(1)} custom-call(f32[48,2048]{1,0:T(8,128)S(1)} %collective-permute-done.6.refs_0_, f32[48,2048]{1,0:T(8,128)S(1)} %collective-permute-done.7.refs_1_, bf16[2048,1536]{1,0:T(8,128)(2,1)S(1)} %get-tuple-element.40.refs_2_.refs_4_, bf16[2048,1536]{1,0:T(8,128)(2,1)S(1)} %get-tuple-element.41.refs_3_.refs_5_), custom_call_target="tpu_custom_call" | custom-call | flops 1811939328 | bytes 786432 | tf_op jit(solution)/shard_map/pallas_call | solution.py:59
  42.5 1.2 %collective-permute-done.12.refs_3_ = f32[48,2048]{1,0:T(8,128)S(1)} collective-permute-done((f32[48,2048]{1,0:T(8,128)S(1)}, f32[48,2048]{1,0:T(8,128)S(1)}, u32[]{:S(2)}, u32[]{:S(2)}) %collective-permute-start.12) | collective-permute-done | bytes 393248 | tf_op jit(solution)/shard_map/ppermute | solution.py:136
  43.8 0.6 collective-permute-done.11.refs_1_
  44.3 3.8 %shard_map.33 = (f32[96,1536]{1,0:T(8,128)S(1)}, f32[96,1536]{1,0:T(8,128)S(1)}) custom-call(f32[48,2048]{1,0:T(8,128)S(1)} %collective-permute-done.4.refs_0_, f32[48,2048]{1,0:T(8,128)S(1)} %collective-permute-done.11.refs_1_, f32[48,2048]{1,0:T(8,128)S(1)} %collective-permute-done.5.refs_2_, f32[48,2048]{1,0:T(8,128)S(1)} %collective-permute-done.12.refs_3_, ...), custom_call_target="tpu_custom_call" | custom-call | flops 3623878656 | bytes 1572864 | tf_op jit(solution)/shard_map/pallas_call | solution.py:59
  48.1 5.8 %collective-permute-done.10.refs_0_ = f32[48,2048]{1,0:T(8,128)S(1)} collective-permute-done((f32[48,2048]{1,0:T(8,128)S(1)}, f32[48,2048]{1,0:T(8,128)S(1)}, u32[]{:S(2)}, u32[]{:S(2)}) %collective-permute-start.10) | collective-permute-done | bytes 393248 | tf_op jit(solution)/shard_map/ppermute | solution.py:136
  54.2 1.7 %collective-permute-start.9 = (f32[48,2048]{1,0:T(8,128)S(1)}, f32[48,2048]{1,0:T(8,128)S(1)}, u32[]{:S(2)}, u32[]{:S(2)}) collective-permute-start(f32[48,2048]{1,0:T(8,128)S(1)} %collective-permute-done.5.refs_2_), channel_id=1, source_target_pairs={{0,16},{1,17},{2,18},{3,19},{4,20},{5,21},{6,22},{7,23},{8,24},{9,... | collective-permute-start | bytes 1179656 | tf_op jit(solution)/shard_map/ppermute | solution.py:136
  56.0 3.1 %shard_map.34 = f32[96,1536]{1,0:T(8,128)S(1)} custom-call(f32[48,2048]{1,0:T(8,128)S(1)} %collective-permute-done.10.refs_0_, f32[48,2048]{1,0:T(8,128)S(1)} %collective-permute-done.13.refs_1_, bf16[2048,1536]{1,0:T(8,128)(2,1)S(1)} %get-tuple-element.40.refs_2_.refs_4_, bf16[2048,1536]{1,0:T(8,128)(2,1)S(1)} %get-tuple-element.41.refs_3_.refs_5_), custom_call_target="tpu_custom_call" | custom-call | flops 1811939328 | bytes 786432 | tf_op jit(solution)/shard_map/pallas_call | solution.py:59
  59.1 6.8 %collective-permute-done.8.refs_0_ = f32[48,2048]{1,0:T(8,128)S(1)} collective-permute-done((f32[48,2048]{1,0:T(8,128)S(1)}, f32[48,2048]{1,0:T(8,128)S(1)}, u32[]{:S(2)}, u32[]{:S(2)}) %collective-permute-start.8) | collective-permute-done | bytes 393248 | tf_op jit(solution)/shard_map/ppermute | solution.py:136
  65.9 8.0 %collective-permute-done.9.refs_2_ = f32[48,2048]{1,0:T(8,128)S(1)} collective-permute-done((f32[48,2048]{1,0:T(8,128)S(1)}, f32[48,2048]{1,0:T(8,128)S(1)}, u32[]{:S(2)}, u32[]{:S(2)}) %collective-permute-start.9) | collective-permute-done | bytes 393248 | tf_op jit(solution)/shard_map/ppermute | solution.py:136
  73.9 0.5 collective-permute-start.14
  74.4 0.5 collective-permute-start.3
  75.4 1.5 %collective-permute-start.22 = (f32[96,1536]{1,0:T(8,128)S(1)}, f32[96,1536]{1,0:T(8,128)S(1)}, u32[]{:S(2)}, u32[]{:S(2)}) collective-permute-start(f32[96,1536]{1,0:T(8,128)S(1)} %shard_map.34), channel_id=1, source_target_pairs={{0,32},{1,33},{2,34},{3,35},{4,36},{5,37},{6,38},{7,39},{8,104},{9... | collective-permute-start | bytes 1769480 | tf_op jit(solution)/shard_map/ppermute | solution.py:136
  77.0 3.8 %shard_map.35 = (f32[96,1536]{1,0:T(8,128)S(1)}, f32[96,1536]{1,0:T(8,128)S(1)}) custom-call(f32[48,2048]{1,0:T(8,128)S(1)} %collective-permute-done.8.refs_0_, f32[48,2048]{1,0:T(8,128)S(1)} %collective-permute-done.14.refs_1_, f32[48,2048]{1,0:T(8,128)S(1)} %collective-permute-done.9.refs_2_, f32[48,2048]{1,0:T(8,128)S(1)} %collective-permute-done.15.refs_3_, ...), custom_call_target="tpu_custom_call" | custom-call | flops 3623878656 | bytes 1572864 | tf_op jit(solution)/shard_map/pallas_call | solution.py:59
  80.8 4.9 %collective-permute-done.3.refs_2_ = f32[48,2048]{1,0:T(8,128)S(1)} collective-permute-done((f32[48,2048]{1,0:T(8,128)S(1)}, f32[48,2048]{1,0:T(8,128)S(1)}, u32[]{:S(2)}, u32[]{:S(2)}) %collective-permute-start.3) | collective-permute-done | bytes 393248 | tf_op jit(solution)/shard_map/ppermute | solution.py:136
  86.2 2.9 %collective-permute-start.18 = (f32[96,1536]{1,0:T(8,128)S(1)}, f32[96,1536]{1,0:T(8,128)S(1)}, u32[]{:S(2)}, u32[]{:S(2)}) collective-permute-start(f32[96,1536]{1,0:T(8,128)S(1)} %get-tuple-element.52), channel_id=1, source_target_pairs={{0,96},{1,97},{2,98},{3,99},{4,100},{5,101},{6,102},{7,103},{8,40}... | collective-permute-start | bytes 1769480 | tf_op jit(solution)/shard_map/ppermute | solution.py:136
  89.3 5.4 %collective-permute-done.22 = f32[96,1536]{1,0:T(8,128)S(1)} collective-permute-done((f32[96,1536]{1,0:T(8,128)S(1)}, f32[96,1536]{1,0:T(8,128)S(1)}, u32[]{:S(2)}, u32[]{:S(2)}) %collective-permute-start.22) | collective-permute-done | bytes 589856 | tf_op jit(solution)/shard_map/ppermute | solution.py:136
  94.7 1.7 %collective-permute-start.21 = (f32[96,1536]{1,0:T(8,128)S(1)}, f32[96,1536]{1,0:T(8,128)S(1)}, u32[]{:S(2)}, u32[]{:S(2)}) collective-permute-start(f32[96,1536]{1,0:T(8,128)S(1)} %get-tuple-element.54), channel_id=1, source_target_pairs={{0,96},{1,97},{2,98},{3,99},{4,100},{5,101},{6,102},{7,103},{8,40}... | collective-permute-start | bytes 1769480 | tf_op jit(solution)/shard_map/ppermute | solution.py:136
  96.9 3.8 %shard_map.36 = (f32[96,1536]{1,0:T(8,128)S(1)}, f32[96,1536]{1,0:T(8,128)S(1)}) custom-call(f32[48,2048]{1,0:T(8,128)S(1)} %shard_map.28.refs_0_, f32[48,2048]{1,0:T(8,128)S(1)} %collective-permute-done.16.refs_1_, f32[48,2048]{1,0:T(8,128)S(1)} %collective-permute-done.3.refs_2_, f32[48,2048]{1,0:T(8,128)S(1)} %collective-permute-done.17.refs_3_, ...), custom_call_target="tpu_custom_call" | custom-call | flops 3623878656 | bytes 1572864 | tf_op jit(solution)/shard_map/pallas_call | solution.py:59
  100.7 2.1 %collective-permute-done.18.refs_1_ = f32[96,1536]{1,0:T(8,128)S(1)} collective-permute-done((f32[96,1536]{1,0:T(8,128)S(1)}, f32[96,1536]{1,0:T(8,128)S(1)}, u32[]{:S(2)}, u32[]{:S(2)}) %collective-permute-start.18) | collective-permute-done | bytes 589856 | tf_op jit(solution)/shard_map/ppermute | solution.py:136
  102.9 4.5 %collective-permute-done.20.refs_2_ = f32[96,1536]{1,0:T(8,128)S(1)} collective-permute-done((f32[96,1536]{1,0:T(8,128)S(1)}, f32[96,1536]{1,0:T(8,128)S(1)}, u32[]{:S(2)}, u32[]{:S(2)}) %collective-permute-start.20) | collective-permute-done | bytes 589856 | tf_op jit(solution)/shard_map/ppermute | solution.py:136
  107.4 8.1 %collective-permute-done.21.refs_4_ = f32[96,1536]{1,0:T(8,128)S(1)} collective-permute-done((f32[96,1536]{1,0:T(8,128)S(1)}, f32[96,1536]{1,0:T(8,128)S(1)}, u32[]{:S(2)}, u32[]{:S(2)}) %collective-permute-start.21) | collective-permute-done | bytes 589856 | tf_op jit(solution)/shard_map/ppermute | solution.py:136
  115.5 2.2 %collective-permute-done.23.refs_5_ = f32[96,1536]{1,0:T(8,128)S(1)} collective-permute-done((f32[96,1536]{1,0:T(8,128)S(1)}, f32[96,1536]{1,0:T(8,128)S(1)}, u32[]{:S(2)}, u32[]{:S(2)}) %collective-permute-start.23) | collective-permute-done | bytes 589856 | tf_op jit(solution)/shard_map/ppermute | solution.py:136
  117.7 1.6 %finish.1 = f32[192,1536]{1,0:T(8,128)} custom-call(s32[1]{0:T(128)} %bitcast.4.col_ref, f32[96,1536]{1,0:T(8,128)S(1)} %get-tuple-element.51.refs_0_, f32[96,1536]{1,0:T(8,128)S(1)} %collective-permute-done.18.refs_1_, f32[96,1536]{1,0:T(8,128)S(1)} %collective-permute-done.20.refs_2_, f32[96,1536]{1,0:T(8,128)S(1)} %get-tuple-element.53.refs_3_, ...), custom_call_target="tpu_custom_call" | custom-call | tf_op jit(solution)/shard_map/finish/pallas_call | solution.py:105
  (30 shorter events, 2.7 us)
Async XLA Ops:
  1.5 3.8 %collective-permute-start = (f32[48,2048]{1,0:T(8,128)S(1)}, f32[48,2048]{1,0:T(8,128)S(1)}, u32[]{:S(2)}, u32[]{:S(2)}) collective-permute-start(f32[48,2048]{1,0:T(8,128)S(1)} %get-tuple-element.33), channel_id=1, source_target_pairs={{0,8},{1,9},{2,10},{3,11},{4,12},{5,13},{6,14},{7,15},{8,0},{9,1},... | collective-permute-start | bytes 1179656 | tf_op jit(solution)/shard_map/ppermute | solution.py:136
  1.6 11.5 %collective-permute-start.1 = (f32[48,2048]{1,0:T(8,128)S(1)}, f32[48,2048]{1,0:T(8,128)S(1)}, u32[]{:S(2)}, u32[]{:S(2)}) collective-permute-start(f32[48,2048]{1,0:T(8,128)S(1)} %get-tuple-element.34), channel_id=1, source_target_pairs={{0,16},{1,17},{2,18},{3,19},{4,20},{5,21},{6,22},{7,23},{8,24},{9,... | collective-permute-start | bytes 1179656 | tf_op jit(solution)/shard_map/ppermute | solution.py:136
  3.3 12.3 %collective-permute-start.2 = (f32[48,2048]{1,0:T(8,128)S(1)}, f32[48,2048]{1,0:T(8,128)S(1)}, u32[]{:S(2)}, u32[]{:S(2)}) collective-permute-start(f32[48,2048]{1,0:T(8,128)S(1)} %get-tuple-element.35), channel_id=1, source_target_pairs={{0,28},{1,29},{2,30},{3,31},{4,24},{5,25},{6,26},{7,27},{8,20},{9,... | collective-permute-start | bytes 1179656 | tf_op jit(solution)/shard_map/ppermute | solution.py:136
  15.7 12.7 %collective-permute-start.6 = (f32[48,2048]{1,0:T(8,128)S(1)}, f32[48,2048]{1,0:T(8,128)S(1)}, u32[]{:S(2)}, u32[]{:S(2)}) collective-permute-start(f32[48,2048]{1,0:T(8,128)S(1)} %shard_map.31), channel_id=1, source_target_pairs={{0,64},{1,65},{2,66},{3,67},{4,68},{5,69},{6,70},{7,71},{8,72},{9,... | collective-permute-start | bytes 1179656 | tf_op jit(solution)/shard_map/ppermute | solution.py:136
  28.4 10.4 %collective-permute-start.7 = (f32[48,2048]{1,0:T(8,128)S(1)}, f32[48,2048]{1,0:T(8,128)S(1)}, u32[]{:S(2)}, u32[]{:S(2)}) collective-permute-start(f32[48,2048]{1,0:T(8,128)S(1)} %collective-permute-done.6.refs_0_), channel_id=1, source_target_pairs={{0,8},{1,9},{2,10},{3,11},{4,12},{5,13},{6,14},{7,15},{8,0},{9,1},... | collective-permute-start | bytes 1179656 | tf_op jit(solution)/shard_map/ppermute | solution.py:136
  28.5 13.5 %collective-permute-start.4 = (f32[48,2048]{1,0:T(8,128)S(1)}, f32[48,2048]{1,0:T(8,128)S(1)}, u32[]{:S(2)}, u32[]{:S(2)}) collective-permute-start(f32[48,2048]{1,0:T(8,128)S(1)} %shard_map.29), channel_id=1, source_target_pairs={{0,96},{1,97},{2,98},{3,99},{4,100},{5,101},{6,102},{7,103},{8,40}... | collective-permute-start | bytes 1179656 | tf_op jit(solution)/shard_map/ppermute | solution.py:136
  31.4 10.6 %collective-permute-start.5 = (f32[48,2048]{1,0:T(8,128)S(1)}, f32[48,2048]{1,0:T(8,128)S(1)}, u32[]{:S(2)}, u32[]{:S(2)}) collective-permute-start(f32[48,2048]{1,0:T(8,128)S(1)} %shard_map.30), channel_id=1, source_target_pairs={{0,32},{1,33},{2,34},{3,35},{4,36},{5,37},{6,38},{7,39},{8,104},{9... | collective-permute-start | bytes 1179656 | tf_op jit(solution)/shard_map/ppermute | solution.py:136
  41.9 1.8 %collective-permute-start.12 = (f32[48,2048]{1,0:T(8,128)S(1)}, f32[48,2048]{1,0:T(8,128)S(1)}, u32[]{:S(2)}, u32[]{:S(2)}) collective-permute-start(f32[48,2048]{1,0:T(8,128)S(1)} %collective-permute-done.4.refs_0_), channel_id=1, source_target_pairs={{0,8},{1,9},{2,10},{3,11},{4,12},{5,13},{6,14},{7,15},{8,0},{9,1},... | collective-permute-start | bytes 1179656 | tf_op jit(solution)/shard_map/ppermute | solution.py:136
  42.4 1.9 %collective-permute-start.11 = (f32[48,2048]{1,0:T(8,128)S(1)}, f32[48,2048]{1,0:T(8,128)S(1)}, u32[]{:S(2)}, u32[]{:S(2)}) collective-permute-start(f32[48,2048]{1,0:T(8,128)S(1)} %collective-permute-done.5.refs_2_), channel_id=1, source_target_pairs={{0,8},{1,9},{2,10},{3,11},{4,12},{5,13},{6,14},{7,15},{8,0},{9,1},... | collective-permute-start | bytes 1179656 | tf_op jit(solution)/shard_map/ppermute | solution.py:136
  42.5 11.4 %collective-permute-start.10 = (f32[48,2048]{1,0:T(8,128)S(1)}, f32[48,2048]{1,0:T(8,128)S(1)}, u32[]{:S(2)}, u32[]{:S(2)}) collective-permute-start(f32[48,2048]{1,0:T(8,128)S(1)} %collective-permute-done.6.refs_0_), channel_id=1, source_target_pairs={{0,16},{1,17},{2,18},{3,19},{4,20},{5,21},{6,22},{7,23},{8,24},{9,... | collective-permute-start | bytes 1179656 | tf_op jit(solution)/shard_map/ppermute | solution.py:136
  53.9 2.0 %collective-permute-start.13 = (f32[48,2048]{1,0:T(8,128)S(1)}, f32[48,2048]{1,0:T(8,128)S(1)}, u32[]{:S(2)}, u32[]{:S(2)}) collective-permute-start(f32[48,2048]{1,0:T(8,128)S(1)} %collective-permute-done.10.refs_0_), channel_id=1, source_target_pairs={{0,8},{1,9},{2,10},{3,11},{4,12},{5,13},{6,14},{7,15},{8,0},{9,1},... | collective-permute-start | bytes 1179656 | tf_op jit(solution)/shard_map/ppermute | solution.py:136
  53.9 12.0 %collective-permute-start.8 = (f32[48,2048]{1,0:T(8,128)S(1)}, f32[48,2048]{1,0:T(8,128)S(1)}, u32[]{:S(2)}, u32[]{:S(2)}) collective-permute-start(f32[48,2048]{1,0:T(8,128)S(1)} %collective-permute-done.4.refs_0_), channel_id=1, source_target_pairs={{0,16},{1,17},{2,18},{3,19},{4,20},{5,21},{6,22},{7,23},{8,24},{9,... | collective-permute-start | bytes 1179656 | tf_op jit(solution)/shard_map/ppermute | solution.py:136
  54.2 19.7 %collective-permute-start.9 = (f32[48,2048]{1,0:T(8,128)S(1)}, f32[48,2048]{1,0:T(8,128)S(1)}, u32[]{:S(2)}, u32[]{:S(2)}) collective-permute-start(f32[48,2048]{1,0:T(8,128)S(1)} %collective-permute-done.5.refs_2_), channel_id=1, source_target_pairs={{0,16},{1,17},{2,18},{3,19},{4,20},{5,21},{6,22},{7,23},{8,24},{9,... | collective-permute-start | bytes 1179656 | tf_op jit(solution)/shard_map/ppermute | solution.py:136
  73.9 3.1 %collective-permute-start.15 = (f32[48,2048]{1,0:T(8,128)S(1)}, f32[48,2048]{1,0:T(8,128)S(1)}, u32[]{:S(2)}, u32[]{:S(2)}) collective-permute-start(f32[48,2048]{1,0:T(8,128)S(1)} %collective-permute-done.8.refs_0_), channel_id=1, source_target_pairs={{0,8},{1,9},{2,10},{3,11},{4,12},{5,13},{6,14},{7,15},{8,0},{9,1},... | collective-permute-start | bytes 1179656 | tf_op jit(solution)/shard_map/ppermute | solution.py:136
  73.9 3.1 %collective-permute-start.14 = (f32[48,2048]{1,0:T(8,128)S(1)}, f32[48,2048]{1,0:T(8,128)S(1)}, u32[]{:S(2)}, u32[]{:S(2)}) collective-permute-start(f32[48,2048]{1,0:T(8,128)S(1)} %collective-permute-done.9.refs_2_), channel_id=1, source_target_pairs={{0,8},{1,9},{2,10},{3,11},{4,12},{5,13},{6,14},{7,15},{8,0},{9,1},... | collective-permute-start | bytes 1179656 | tf_op jit(solution)/shard_map/ppermute | solution.py:136
  74.4 11.3 %collective-permute-start.3 = (f32[48,2048]{1,0:T(8,128)S(1)}, f32[48,2048]{1,0:T(8,128)S(1)}, u32[]{:S(2)}, u32[]{:S(2)}) collective-permute-start(f32[48,2048]{1,0:T(8,128)S(1)} %shard_map.28.refs_0_), channel_id=1, source_target_pairs={{0,16},{1,17},{2,18},{3,19},{4,20},{5,21},{6,22},{7,23},{8,24},{9,... | collective-permute-start | bytes 1179656 | tf_op jit(solution)/shard_map/ppermute | solution.py:136
  75.0 14.2 %collective-permute-start.19 = (f32[96,1536]{1,0:T(8,128)S(1)}, f32[96,1536]{1,0:T(8,128)S(1)}, u32[]{:S(2)}, u32[]{:S(2)}) collective-permute-start(f32[96,1536]{1,0:T(8,128)S(1)} %shard_map.32), channel_id=1, source_target_pairs={{0,32},{1,33},{2,34},{3,35},{4,36},{5,37},{6,38},{7,39},{8,104},{9... | collective-permute-start | bytes 1769480 | tf_op jit(solution)/shard_map/ppermute | solution.py:136
  75.4 19.3 %collective-permute-start.22 = (f32[96,1536]{1,0:T(8,128)S(1)}, f32[96,1536]{1,0:T(8,128)S(1)}, u32[]{:S(2)}, u32[]{:S(2)}) collective-permute-start(f32[96,1536]{1,0:T(8,128)S(1)} %shard_map.34), channel_id=1, source_target_pairs={{0,32},{1,33},{2,34},{3,35},{4,36},{5,37},{6,38},{7,39},{8,104},{9... | collective-permute-start | bytes 1769480 | tf_op jit(solution)/shard_map/ppermute | solution.py:136
  85.7 10.8 %collective-permute-start.16 = (f32[48,2048]{1,0:T(8,128)S(1)}, f32[48,2048]{1,0:T(8,128)S(1)}, u32[]{:S(2)}, u32[]{:S(2)}) collective-permute-start(f32[48,2048]{1,0:T(8,128)S(1)} %shard_map.28.refs_0_), channel_id=1, source_target_pairs={{0,8},{1,9},{2,10},{3,11},{4,12},{5,13},{6,14},{7,15},{8,0},{9,1},... | collective-permute-start | bytes 1179656 | tf_op jit(solution)/shard_map/ppermute | solution.py:136
  85.7 11.2 %collective-permute-start.17 = (f32[48,2048]{1,0:T(8,128)S(1)}, f32[48,2048]{1,0:T(8,128)S(1)}, u32[]{:S(2)}, u32[]{:S(2)}) collective-permute-start(f32[48,2048]{1,0:T(8,128)S(1)} %collective-permute-done.3.refs_2_), channel_id=1, source_target_pairs={{0,8},{1,9},{2,10},{3,11},{4,12},{5,13},{6,14},{7,15},{8,0},{9,1},... | collective-permute-start | bytes 1179656 | tf_op jit(solution)/shard_map/ppermute | solution.py:136
  86.2 16.6 %collective-permute-start.18 = (f32[96,1536]{1,0:T(8,128)S(1)}, f32[96,1536]{1,0:T(8,128)S(1)}, u32[]{:S(2)}, u32[]{:S(2)}) collective-permute-start(f32[96,1536]{1,0:T(8,128)S(1)} %get-tuple-element.52), channel_id=1, source_target_pairs={{0,96},{1,97},{2,98},{3,99},{4,100},{5,101},{6,102},{7,103},{8,40}... | collective-permute-start | bytes 1769480 | tf_op jit(solution)/shard_map/ppermute | solution.py:136
  89.2 18.2 %collective-permute-start.20 = (f32[96,1536]{1,0:T(8,128)S(1)}, f32[96,1536]{1,0:T(8,128)S(1)}, u32[]{:S(2)}, u32[]{:S(2)}) collective-permute-start(f32[96,1536]{1,0:T(8,128)S(1)} %add.71), channel_id=1, source_target_pairs={{0,32},{1,33},{2,34},{3,35},{4,36},{5,37},{6,38},{7,39},{8,104},{9... | collective-permute-start | bytes 1769480 | tf_op jit(solution)/shard_map/ppermute | solution.py:136
  94.7 20.8 %collective-permute-start.21 = (f32[96,1536]{1,0:T(8,128)S(1)}, f32[96,1536]{1,0:T(8,128)S(1)}, u32[]{:S(2)}, u32[]{:S(2)}) collective-permute-start(f32[96,1536]{1,0:T(8,128)S(1)} %get-tuple-element.54), channel_id=1, source_target_pairs={{0,96},{1,97},{2,98},{3,99},{4,100},{5,101},{6,102},{7,103},{8,40}... | collective-permute-start | bytes 1769480 | tf_op jit(solution)/shard_map/ppermute | solution.py:136
  96.5 21.1 %collective-permute-start.23 = (f32[96,1536]{1,0:T(8,128)S(1)}, f32[96,1536]{1,0:T(8,128)S(1)}, u32[]{:S(2)}, u32[]{:S(2)}) collective-permute-start(f32[96,1536]{1,0:T(8,128)S(1)} %add.72), channel_id=1, source_target_pairs={{0,32},{1,33},{2,34},{3,35},{4,36},{5,37},{6,38},{7,39},{8,104},{9... | collective-permute-start | bytes 1769480 | tf_op jit(solution)/shard_map/ppermute | solution.py:136

commit v2 on v1

--- a/solution.py
+++ b/solution.py
@@ -37,14 +37,30 @@
     )(pltpu.with_memory_space_constraint(b, pltpu.HBM))
 
 
+def hold_kernel(in_ref, out_ref):
+    out_ref[0] = in_ref[0]
+
+
+def hold(value):
+    smem = pl.BlockSpec(memory_space=pltpu.SMEM)
+    return pl.pallas_call(
+        hold_kernel,
+        in_specs=[smem],
+        out_specs=smem,
+        out_shape=jax.ShapeDtypeStruct(value.shape, value.dtype),
+        compiler_params=pltpu.CompilerParams(vmem_limit_bytes=1 << 20),
+        name="hold",
+    )(value)
+
+
 def multiply_kernel(count, *refs):
-    pieces, (high_ref, low_ref), outs = refs[:count], refs[count : count + 2], refs[count + 2 :]
+    pieces, (b_high, b_low), outs = refs[:count], refs[count : count + 2], refs[count + 2 :]
     high, low = split(jnp.concatenate([piece[...] for piece in pieces], 0))
     dot = functools.partial(jnp.dot, preferred_element_type=jnp.float32)
     size = outs[0].shape[0]
-    for start in range(0, high_ref.shape[1], BLOCK):
+    for start in range(0, b_high.shape[1], BLOCK):
         at = slice(start, start + BLOCK)
-        result = dot(high, high_ref[:, at]) + dot(high, low_ref[:, at]) + dot(low, high_ref[:, at])
+        result = dot(high, b_high[:, at]) + dot(high, b_low[:, at]) + dot(low, b_high[:, at])
         for i, out in enumerate(outs):
             out[:, at] = result[i * size : (i + 1) * size]
 
@@ -53,8 +69,8 @@
     return [pltpu.with_memory_space_constraint(v, pltpu.VMEM) for v in values]
 
 
-def multiply(pieces, b_high, b_low):
-    (size, depth), width = pieces[0].shape, b_high.shape[1]
+def multiply(pieces, split_b):
+    (size, depth), width = pieces[0].shape, split_b[0].shape[1]
     rows, results = size * len(pieces), len(pieces) // 2
     return pl.pallas_call(
         functools.partial(multiply_kernel, len(pieces)),
@@ -65,7 +81,7 @@
         cost_estimate=pl.CostEstimate(
             flops=6 * rows * depth * width, bytes_accessed=4 * rows * depth, transcendentals=0
         ),
-    )(*in_vmem(pieces), b_high, b_low)
+    )(*in_vmem(pieces), *split_b)
 
 
 def choose_kernel(which_ref, *refs):
@@ -87,33 +103,26 @@
 
 
 def finish_kernel(col_ref, *refs):
-    i, out = pl.program_id(0), refs[-1]
-    at = pl.ds(i % 2 * out.shape[0], out.shape[0])
-    early, late = refs[:3], refs[3:6]
-
-    @pl.when(i < 2)
-    def _():
-        out[...] = early[0][at, :] + early[1][at, :] + early[2][at, :]
-
-    @pl.when(i >= 2)
-    def _():
-        out[...] = late[0][at, :] + late[1][at, :] + late[2][at, :]
-
-
-def finish(col, early, late):
-    rows, width = early[0].shape
+    out = refs[-1]
+    at = pl.ds(pl.program_id(0) * out.shape[0], out.shape[0])
+    out[...] = refs[0][at, :] + refs[1][at, :] + refs[2][at, :]
+
+
+def finish(part, col, values, into=None):
+    rows, width = values[0].shape
+    given = () if into is None else (into,)
     return pl.pallas_call(
         finish_kernel,
         grid_spec=pltpu.PrefetchScalarGridSpec(
             num_scalar_prefetch=1,
-            grid=(4,),
-            in_specs=[VMEM] * 6,
-            out_specs=pl.BlockSpec((rows // 2, width), lambda i, col: (i ^ col[0], 0)),
+            grid=(2,),
+            in_specs=[VMEM] * 3 + [pl.BlockSpec(memory_space=pl.ANY)] * len(given),
+            out_specs=pl.BlockSpec((rows // 2, width), lambda i, col: ((i + 2 * part) ^ col[0], 0)),
         ),
         out_shape=jax.ShapeDtypeStruct((2 * rows, width), jnp.float32),
+        input_output_aliases={4: 0} if given else {},
         compiler_params=pltpu.CompilerParams(vmem_limit_bytes=8 << 20),
-        name="finish",
-    )(col, *in_vmem(early + late))
+    )(col, *in_vmem(values), *given)
 
 
 def after(values, anchors):
@@ -152,8 +161,8 @@
     scalars, taken, right_factor = lax.optimization_barrier((scalars, taken, right_factor))
     source2, source_p, source_q, source0, col = scalars
 
-    b_high, b_low = prepare(right_factor)
-    mul = lambda pieces: multiply(pieces, b_high, b_low)
+    split_b = prepare(right_factor)
+    mul = lambda pieces: multiply(pieces, split_b)
 
     spread = [
         taken[0],
@@ -204,7 +213,8 @@
     own_e, own_l = mul([mine0, near0, across0, far0])
     from_p_l = send(p_l + first_l, forward)
 
-    return finish(col, [own_e, from_q_e, from_p_e], [own_l, from_q_l, from_p_l])
+    result = finish(0, hold(col), [own_e, from_q_e, from_p_e])
+    return finish(1, col, [own_l, from_q_l, from_p_l], result)
 
 
 def solution(mesh):

time: 120 us -> 119 us (level)
  waiting for transfers between devices: 69.7 us -> 67.8 us
    ppermute x24, waiting for transfers between devices: 69.7 us -> 67.8 us  [send(): return lax.ppermute(value, AXES, pairs)]
  transfers between devices with their start and end apart: 24 -> 24, of which waited for: 14 -> 14; matrix products, arithmetic and copies ran while one was open for 0% -> 0% of each run, Pallas kernels for 21% -> 23%
where the time goes in v2:
time: 119 us
  waiting for transfers between devices  67.8 us (57%)
  Pallas kernels  28 us (24%)
  starting transfers between devices  21 us (18%)
  local copies, waits for them, and re-layouts  1.47 us (1%)
    ppermute x24, waiting for transfers between devices, send(): return lax.ppermute(value, AXES, pairs)  67.8 us
    ppermute x24, starting transfers between devices, send(): return lax.ppermute(value, AXES, pairs)  21 us
    pallas_call x5, Pallas kernels, multiply(): pl.pallas_call(functools.partial(multiply_kernel, len(pieces)), in_specs=...  17.7 us
    pallas_call x1, Pallas kernels, prepare(): pl.pallas_call(prepare_kernel, grid=(depth // BLOCK,), in_specs=[pl.Block...  7.33 us
  transfers between devices with their start and end apart: 24, of which 14 were waited for; matrix products, arithmetic and copies ran while one was open for 0% of the time, Pallas kernels for 23%

profile of v2, /device:TPU:0, one launch (start us, length us, event | category | flops | bytes accessed | tf_op | source)
XLA Modules:
  0.0 118.7 jit_solution(8635353906555960915)
XLA Ops:
  0.0 1.5 %constant_dynamic-slice_fusion = (f32[48,2048]{1,0:T(8,128)S(1)}, f32[48,2048]{1,0:T(8,128)S(1)}, f32[48,2048]{1,0:T(8,128)S(1)}, f32[48,2048]{1,0:T(8,128)S(1)}) fusion(f32[1536,2048]{1,0:T(8,128)} %param.2, s32[]{:T(128)S(6)} %select_n.48, s32[]{:T(128)S(6)} %select_n.46, s32[]{:T(128)S(6)} %select_n.45, s32[]{:T(128)S(6)} %select_n.47), kind=kLoop, calls=%fused_computation | loop fusion | bytes 3145744 | tf_op jit(solution)/shard_map/dynamic_slice | solution.py:155
  1.6 1.8 %collective-permute-start.1 = (f32[48,2048]{1,0:T(8,128)S(1)}, f32[48,2048]{1,0:T(8,128)S(1)}, u32[]{:S(2)}, u32[]{:S(2)}) collective-permute-start(f32[48,2048]{1,0:T(8,128)S(1)} %get-tuple-element.34), channel_id=1, source_target_pairs={{0,16},{1,17},{2,18},{3,19},{4,20},{5,21},{6,22},{7,23},{8,24},{9,... | collective-permute-start | bytes 1179656 | tf_op jit(solution)/shard_map/ppermute | solution.py:145
  3.3 1.9 %collective-permute-start.2 = (f32[48,2048]{1,0:T(8,128)S(1)}, f32[48,2048]{1,0:T(8,128)S(1)}, u32[]{:S(2)}, u32[]{:S(2)}) collective-permute-start(f32[48,2048]{1,0:T(8,128)S(1)} %get-tuple-element.35), channel_id=1, source_target_pairs={{0,28},{1,29},{2,30},{3,31},{4,24},{5,25},{6,26},{7,27},{8,20},{9,... | collective-permute-start | bytes 1179656 | tf_op jit(solution)/shard_map/ppermute | solution.py:145
  5.3 7.8 %collective-permute-done.1.refs_2_ = f32[48,2048]{1,0:T(8,128)S(1)} collective-permute-done((f32[48,2048]{1,0:T(8,128)S(1)}, f32[48,2048]{1,0:T(8,128)S(1)}, u32[]{:S(2)}, u32[]{:S(2)}) %collective-permute-start.1) | collective-permute-done | bytes 393248 | tf_op jit(solution)/shard_map/ppermute | solution.py:145
  13.1 2.6 %collective-permute-done.2.refs_3_ = f32[48,2048]{1,0:T(8,128)S(1)} collective-permute-done((f32[48,2048]{1,0:T(8,128)S(1)}, f32[48,2048]{1,0:T(8,128)S(1)}, u32[]{:S(2)}, u32[]{:S(2)}) %collective-permute-start.2) | collective-permute-done | bytes 393248 | tf_op jit(solution)/shard_map/ppermute | solution.py:145
  15.7 3.1 %collective-permute-start.6 = (f32[48,2048]{1,0:T(8,128)S(1)}, f32[48,2048]{1,0:T(8,128)S(1)}, u32[]{:S(2)}, u32[]{:S(2)}) collective-permute-start(f32[48,2048]{1,0:T(8,128)S(1)} %shard_map.31), channel_id=1, source_target_pairs={{0,64},{1,65},{2,66},{3,67},{4,68},{5,69},{6,70},{7,71},{8,72},{9,... | collective-permute-start | bytes 1179656 | tf_op jit(solution)/shard_map/ppermute | solution.py:145
  18.8 9.6 %collective-permute-done.6.refs_0_ = f32[48,2048]{1,0:T(8,128)S(1)} collective-permute-done((f32[48,2048]{1,0:T(8,128)S(1)}, f32[48,2048]{1,0:T(8,128)S(1)}, u32[]{:S(2)}, u32[]{:S(2)}) %collective-permute-start.6) | collective-permute-done | bytes 393248 | tf_op jit(solution)/shard_map/ppermute | solution.py:145
  28.5 1.6 %collective-permute-start.5 = (f32[48,2048]{1,0:T(8,128)S(1)}, f32[48,2048]{1,0:T(8,128)S(1)}, u32[]{:S(2)}, u32[]{:S(2)}) collective-permute-start(f32[48,2048]{1,0:T(8,128)S(1)} %shard_map.30), channel_id=1, source_target_pairs={{0,32},{1,33},{2,34},{3,35},{4,36},{5,37},{6,38},{7,39},{8,104},{9... | collective-permute-start | bytes 1179656 | tf_op jit(solution)/shard_map/ppermute | solution.py:145
  30.1 1.8 %collective-permute-start.4 = (f32[48,2048]{1,0:T(8,128)S(1)}, f32[48,2048]{1,0:T(8,128)S(1)}, u32[]{:S(2)}, u32[]{:S(2)}) collective-permute-start(f32[48,2048]{1,0:T(8,128)S(1)} %shard_map.29), channel_id=1, source_target_pairs={{0,96},{1,97},{2,98},{3,99},{4,100},{5,101},{6,102},{7,103},{8,40}... | collective-permute-start | bytes 1179656 | tf_op jit(solution)/shard_map/ppermute | solution.py:145
  31.9 7.3 %prepare.1 = (bf16[2048,1536]{1,0:T(8,128)(2,1)S(1)}, bf16[2048,1536]{1,0:T(8,128)(2,1)S(1)}) custom-call(f32[2048,1536]{1,0:T(8,128)} %b_ref), custom_call_target="tpu_custom_call" | custom-call | tf_op jit(solution)/shard_map/prepare/pallas_call | solution.py:29
  39.2 3.1 %shard_map.32 = f32[96,1536]{1,0:T(8,128)S(1)} custom-call(f32[48,2048]{1,0:T(8,128)S(1)} %collective-permute-done.6.refs_0_, f32[48,2048]{1,0:T(8,128)S(1)} %collective-permute-done.7.refs_1_, bf16[2048,1536]{1,0:T(8,128)(2,1)S(1)} %get-tuple-element.40.refs_2_.refs_4_, bf16[2048,1536]{1,0:T(8,128)(2,1)S(1)} %get-tuple-element.41.refs_3_.refs_5_), custom_call_target="tpu_custom_call" | custom-call | flops 1811939328 | bytes 786432 | tf_op jit(solution)/shard_map/pallas_call | solution.py:75
  43.0 1.2 %collective-permute-done.11.refs_1_ = f32[48,2048]{1,0:T(8,128)S(1)} collective-permute-done((f32[48,2048]{1,0:T(8,128)S(1)}, f32[48,2048]{1,0:T(8,128)S(1)}, u32[]{:S(2)}, u32[]{:S(2)}) %collective-permute-start.11) | collective-permute-done | bytes 393248 | tf_op jit(solution)/shard_map/ppermute | solution.py:145
  44.7 3.8 %shard_map.33 = (f32[96,1536]{1,0:T(8,128)S(1)}, f32[96,1536]{1,0:T(8,128)S(1)}) custom-call(f32[48,2048]{1,0:T(8,128)S(1)} %collective-permute-done.4.refs_0_, f32[48,2048]{1,0:T(8,128)S(1)} %collective-permute-done.11.refs_1_, f32[48,2048]{1,0:T(8,128)S(1)} %collective-permute-done.5.refs_2_, f32[48,2048]{1,0:T(8,128)S(1)} %collective-permute-done.12.refs_3_, ...), custom_call_target="tpu_custom_call" | custom-call | flops 3623878656 | bytes 1572864 | tf_op jit(solution)/shard_map/pallas_call | solution.py:75
  48.6 5.5 %collective-permute-done.10.refs_0_ = f32[48,2048]{1,0:T(8,128)S(1)} collective-permute-done((f32[48,2048]{1,0:T(8,128)S(1)}, f32[48,2048]{1,0:T(8,128)S(1)}, u32[]{:S(2)}, u32[]{:S(2)}) %collective-permute-start.10) | collective-permute-done | bytes 393248 | tf_op jit(solution)/shard_map/ppermute | solution.py:145
  54.4 1.7 %collective-permute-start.9 = (f32[48,2048]{1,0:T(8,128)S(1)}, f32[48,2048]{1,0:T(8,128)S(1)}, u32[]{:S(2)}, u32[]{:S(2)}) collective-permute-start(f32[48,2048]{1,0:T(8,128)S(1)} %collective-permute-done.5.refs_2_), channel_id=1, source_target_pairs={{0,16},{1,17},{2,18},{3,19},{4,20},{5,21},{6,22},{7,23},{8,24},{9,... | collective-permute-start | bytes 1179656 | tf_op jit(solution)/shard_map/ppermute | solution.py:145
  56.1 3.1 %shard_map.34 = f32[96,1536]{1,0:T(8,128)S(1)} custom-call(f32[48,2048]{1,0:T(8,128)S(1)} %collective-permute-done.10.refs_0_, f32[48,2048]{1,0:T(8,128)S(1)} %collective-permute-done.13.refs_1_, bf16[2048,1536]{1,0:T(8,128)(2,1)S(1)} %get-tuple-element.40.refs_2_.refs_4_, bf16[2048,1536]{1,0:T(8,128)(2,1)S(1)} %get-tuple-element.41.refs_3_.refs_5_), custom_call_target="tpu_custom_call" | custom-call | flops 1811939328 | bytes 786432 | tf_op jit(solution)/shard_map/pallas_call | solution.py:75
  59.2 6.8 %collective-permute-done.8.refs_0_ = f32[48,2048]{1,0:T(8,128)S(1)} collective-permute-done((f32[48,2048]{1,0:T(8,128)S(1)}, f32[48,2048]{1,0:T(8,128)S(1)}, u32[]{:S(2)}, u32[]{:S(2)}) %collective-permute-start.8) | collective-permute-done | bytes 393248 | tf_op jit(solution)/shard_map/ppermute | solution.py:145
  66.1 8.0 %collective-permute-done.9.refs_2_ = f32[48,2048]{1,0:T(8,128)S(1)} collective-permute-done((f32[48,2048]{1,0:T(8,128)S(1)}, f32[48,2048]{1,0:T(8,128)S(1)}, u32[]{:S(2)}, u32[]{:S(2)}) %collective-permute-start.9) | collective-permute-done | bytes 393248 | tf_op jit(solution)/shard_map/ppermute | solution.py:145
  75.4 1.5 %collective-permute-start.19 = (f32[96,1536]{1,0:T(8,128)S(1)}, f32[96,1536]{1,0:T(8,128)S(1)}, u32[]{:S(2)}, u32[]{:S(2)}) collective-permute-start(f32[96,1536]{1,0:T(8,128)S(1)} %shard_map.34), channel_id=1, source_target_pairs={{0,32},{1,33},{2,34},{3,35},{4,36},{5,37},{6,38},{7,39},{8,104},{9... | collective-permute-start | bytes 1769480 | tf_op jit(solution)/shard_map/ppermute | solution.py:145
  76.9 3.8 %shard_map.35 = (f32[96,1536]{1,0:T(8,128)S(1)}, f32[96,1536]{1,0:T(8,128)S(1)}) custom-call(f32[48,2048]{1,0:T(8,128)S(1)} %collective-permute-done.8.refs_0_, f32[48,2048]{1,0:T(8,128)S(1)} %collective-permute-done.14.refs_1_, f32[48,2048]{1,0:T(8,128)S(1)} %collective-permute-done.9.refs_2_, f32[48,2048]{1,0:T(8,128)S(1)} %collective-permute-done.15.refs_3_, ...), custom_call_target="tpu_custom_call" | custom-call | flops 3623878656 | bytes 1572864 | tf_op jit(solution)/shard_map/pallas_call | solution.py:75
  80.7 5.1 %collective-permute-done.3.refs_2_ = f32[48,2048]{1,0:T(8,128)S(1)} collective-permute-done((f32[48,2048]{1,0:T(8,128)S(1)}, f32[48,2048]{1,0:T(8,128)S(1)}, u32[]{:S(2)}, u32[]{:S(2)}) %collective-permute-start.3) | collective-permute-done | bytes 393248 | tf_op jit(solution)/shard_map/ppermute | solution.py:145
  86.4 2.6 %collective-permute-start.21 = (f32[96,1536]{1,0:T(8,128)S(1)}, f32[96,1536]{1,0:T(8,128)S(1)}, u32[]{:S(2)}, u32[]{:S(2)}) collective-permute-start(f32[96,1536]{1,0:T(8,128)S(1)} %get-tuple-element.54), channel_id=1, source_target_pairs={{0,96},{1,97},{2,98},{3,99},{4,100},{5,101},{6,102},{7,103},{8,40}... | collective-permute-start | bytes 1769480 | tf_op jit(solution)/shard_map/ppermute | solution.py:145
  89.2 5.7 %collective-permute-done.19 = f32[96,1536]{1,0:T(8,128)S(1)} collective-permute-done((f32[96,1536]{1,0:T(8,128)S(1)}, f32[96,1536]{1,0:T(8,128)S(1)}, u32[]{:S(2)}, u32[]{:S(2)}) %collective-permute-start.19) | collective-permute-done | bytes 589856 | tf_op jit(solution)/shard_map/ppermute | solution.py:145
  94.9 1.4 %collective-permute-start.18 = (f32[96,1536]{1,0:T(8,128)S(1)}, f32[96,1536]{1,0:T(8,128)S(1)}, u32[]{:S(2)}, u32[]{:S(2)}) collective-permute-start(f32[96,1536]{1,0:T(8,128)S(1)} %get-tuple-element.52), channel_id=1, source_target_pairs={{0,96},{1,97},{2,98},{3,99},{4,100},{5,101},{6,102},{7,103},{8,40}... | collective-permute-start | bytes 1769480 | tf_op jit(solution)/shard_map/ppermute | solution.py:145
  96.4 0.7 collective-permute-start.20
  97.6 3.8 %shard_map.36 = (f32[96,1536]{1,0:T(8,128)S(1)}, f32[96,1536]{1,0:T(8,128)S(1)}) custom-call(f32[48,2048]{1,0:T(8,128)S(1)} %shard_map.28.refs_0_, f32[48,2048]{1,0:T(8,128)S(1)} %collective-permute-done.16.refs_1_, f32[48,2048]{1,0:T(8,128)S(1)} %collective-permute-done.3.refs_2_, f32[48,2048]{1,0:T(8,128)S(1)} %collective-permute-done.17.refs_3_, ...), custom_call_target="tpu_custom_call" | custom-call | flops 3623878656 | bytes 1572864 | tf_op jit(solution)/shard_map/pallas_call | solution.py:75
  101.4 1.3 %collective-permute-done.21.refs_1_ = f32[96,1536]{1,0:T(8,128)S(1)} collective-permute-done((f32[96,1536]{1,0:T(8,128)S(1)}, f32[96,1536]{1,0:T(8,128)S(1)}, u32[]{:S(2)}, u32[]{:S(2)}) %collective-permute-start.21) | collective-permute-done | bytes 589856 | tf_op jit(solution)/shard_map/ppermute | solution.py:145
  102.7 4.8 %collective-permute-done.23.refs_2_ = f32[96,1536]{1,0:T(8,128)S(1)} collective-permute-done((f32[96,1536]{1,0:T(8,128)S(1)}, f32[96,1536]{1,0:T(8,128)S(1)}, u32[]{:S(2)}, u32[]{:S(2)}) %collective-permute-start.23) | collective-permute-done | bytes 589856 | tf_op jit(solution)/shard_map/ppermute | solution.py:145
  107.5 1.5 %shard_map.37.refs_3_ = f32[192,1536]{1,0:T(8,128)} custom-call(s32[1]{0:T(128)} %hold.1.col_ref, f32[96,1536]{1,0:T(8,128)S(1)} %get-tuple-element.53.refs_0_, f32[96,1536]{1,0:T(8,128)S(1)} %collective-permute-done.21.refs_1_, f32[96,1536]{1,0:T(8,128)S(1)} %collective-permute-done.23.refs_2_), custom_call_target="tpu_custom_call" | custom-call | tf_op jit(solution)/shard_map/pallas_call | solution.py:114
  109.0 6.3 %collective-permute-done.18.refs_1_ = f32[96,1536]{1,0:T(8,128)S(1)} collective-permute-done((f32[96,1536]{1,0:T(8,128)S(1)}, f32[96,1536]{1,0:T(8,128)S(1)}, u32[]{:S(2)}, u32[]{:S(2)}) %collective-permute-start.18) | collective-permute-done | bytes 589856 | tf_op jit(solution)/shard_map/ppermute | solution.py:145
  115.4 2.5 %collective-permute-done.20.refs_2_ = f32[96,1536]{1,0:T(8,128)S(1)} collective-permute-done((f32[96,1536]{1,0:T(8,128)S(1)}, f32[96,1536]{1,0:T(8,128)S(1)}, u32[]{:S(2)}, u32[]{:S(2)}) %collective-permute-start.20) | collective-permute-done | bytes 589856 | tf_op jit(solution)/shard_map/ppermute | solution.py:145
  117.8 0.9 shard_map.38
  (32 shorter events, 4.2 us)
Async XLA Ops:
  1.5 3.8 %collective-permute-start = (f32[48,2048]{1,0:T(8,128)S(1)}, f32[48,2048]{1,0:T(8,128)S(1)}, u32[]{:S(2)}, u32[]{:S(2)}) collective-permute-start(f32[48,2048]{1,0:T(8,128)S(1)} %get-tuple-element.33), channel_id=1, source_target_pairs={{0,8},{1,9},{2,10},{3,11},{4,12},{5,13},{6,14},{7,15},{8,0},{9,1},... | collective-permute-start | bytes 1179656 | tf_op jit(solution)/shard_map/ppermute | solution.py:145
  1.6 11.5 %collective-permute-start.1 = (f32[48,2048]{1,0:T(8,128)S(1)}, f32[48,2048]{1,0:T(8,128)S(1)}, u32[]{:S(2)}, u32[]{:S(2)}) collective-permute-start(f32[48,2048]{1,0:T(8,128)S(1)} %get-tuple-element.34), channel_id=1, source_target_pairs={{0,16},{1,17},{2,18},{3,19},{4,20},{5,21},{6,22},{7,23},{8,24},{9,... | collective-permute-start | bytes 1179656 | tf_op jit(solution)/shard_map/ppermute | solution.py:145
  3.3 12.3 %collective-permute-start.2 = (f32[48,2048]{1,0:T(8,128)S(1)}, f32[48,2048]{1,0:T(8,128)S(1)}, u32[]{:S(2)}, u32[]{:S(2)}) collective-permute-start(f32[48,2048]{1,0:T(8,128)S(1)} %get-tuple-element.35), channel_id=1, source_target_pairs={{0,28},{1,29},{2,30},{3,31},{4,24},{5,25},{6,26},{7,27},{8,20},{9,... | collective-permute-start | bytes 1179656 | tf_op jit(solution)/shard_map/ppermute | solution.py:145
  15.7 12.7 %collective-permute-start.6 = (f32[48,2048]{1,0:T(8,128)S(1)}, f32[48,2048]{1,0:T(8,128)S(1)}, u32[]{:S(2)}, u32[]{:S(2)}) collective-permute-start(f32[48,2048]{1,0:T(8,128)S(1)} %shard_map.31), channel_id=1, source_target_pairs={{0,64},{1,65},{2,66},{3,67},{4,68},{5,69},{6,70},{7,71},{8,72},{9,... | collective-permute-start | bytes 1179656 | tf_op jit(solution)/shard_map/ppermute | solution.py:145
  28.4 10.8 %collective-permute-start.7 = (f32[48,2048]{1,0:T(8,128)S(1)}, f32[48,2048]{1,0:T(8,128)S(1)}, u32[]{:S(2)}, u32[]{:S(2)}) collective-permute-start(f32[48,2048]{1,0:T(8,128)S(1)} %collective-permute-done.6.refs_0_), channel_id=1, source_target_pairs={{0,8},{1,9},{2,10},{3,11},{4,12},{5,13},{6,14},{7,15},{8,0},{9,1},... | collective-permute-start | bytes 1179656 | tf_op jit(solution)/shard_map/ppermute | solution.py:145
  28.5 13.9 %collective-permute-start.5 = (f32[48,2048]{1,0:T(8,128)S(1)}, f32[48,2048]{1,0:T(8,128)S(1)}, u32[]{:S(2)}, u32[]{:S(2)}) collective-permute-start(f32[48,2048]{1,0:T(8,128)S(1)} %shard_map.30), channel_id=1, source_target_pairs={{0,32},{1,33},{2,34},{3,35},{4,36},{5,37},{6,38},{7,39},{8,104},{9... | collective-permute-start | bytes 1179656 | tf_op jit(solution)/shard_map/ppermute | solution.py:145
  30.1 12.3 %collective-permute-start.4 = (f32[48,2048]{1,0:T(8,128)S(1)}, f32[48,2048]{1,0:T(8,128)S(1)}, u32[]{:S(2)}, u32[]{:S(2)}) collective-permute-start(f32[48,2048]{1,0:T(8,128)S(1)} %shard_map.29), channel_id=1, source_target_pairs={{0,96},{1,97},{2,98},{3,99},{4,100},{5,101},{6,102},{7,103},{8,40}... | collective-permute-start | bytes 1179656 | tf_op jit(solution)/shard_map/ppermute | solution.py:145
  42.4 1.8 %collective-permute-start.11 = (f32[48,2048]{1,0:T(8,128)S(1)}, f32[48,2048]{1,0:T(8,128)S(1)}, u32[]{:S(2)}, u32[]{:S(2)}) collective-permute-start(f32[48,2048]{1,0:T(8,128)S(1)} %collective-permute-done.5.refs_2_), channel_id=1, source_target_pairs={{0,8},{1,9},{2,10},{3,11},{4,12},{5,13},{6,14},{7,15},{8,0},{9,1},... | collective-permute-start | bytes 1179656 | tf_op jit(solution)/shard_map/ppermute | solution.py:145
  42.5 2.3 %collective-permute-start.12 = (f32[48,2048]{1,0:T(8,128)S(1)}, f32[48,2048]{1,0:T(8,128)S(1)}, u32[]{:S(2)}, u32[]{:S(2)}) collective-permute-start(f32[48,2048]{1,0:T(8,128)S(1)} %collective-permute-done.4.refs_0_), channel_id=1, source_target_pairs={{0,8},{1,9},{2,10},{3,11},{4,12},{5,13},{6,14},{7,15},{8,0},{9,1},... | collective-permute-start | bytes 1179656 | tf_op jit(solution)/shard_map/ppermute | solution.py:145
  43.0 11.1 %collective-permute-start.10 = (f32[48,2048]{1,0:T(8,128)S(1)}, f32[48,2048]{1,0:T(8,128)S(1)}, u32[]{:S(2)}, u32[]{:S(2)}) collective-permute-start(f32[48,2048]{1,0:T(8,128)S(1)} %collective-permute-done.6.refs_0_), channel_id=1, source_target_pairs={{0,16},{1,17},{2,18},{3,19},{4,20},{5,21},{6,22},{7,23},{8,24},{9,... | collective-permute-start | bytes 1179656 | tf_op jit(solution)/shard_map/ppermute | solution.py:145
  54.1 2.0 %collective-permute-start.13 = (f32[48,2048]{1,0:T(8,128)S(1)}, f32[48,2048]{1,0:T(8,128)S(1)}, u32[]{:S(2)}, u32[]{:S(2)}) collective-permute-start(f32[48,2048]{1,0:T(8,128)S(1)} %collective-permute-done.10.refs_0_), channel_id=1, source_target_pairs={{0,8},{1,9},{2,10},{3,11},{4,12},{5,13},{6,14},{7,15},{8,0},{9,1},... | collective-permute-start | bytes 1179656 | tf_op jit(solution)/shard_map/ppermute | solution.py:145
  54.1 12.0 %collective-permute-start.8 = (f32[48,2048]{1,0:T(8,128)S(1)}, f32[48,2048]{1,0:T(8,128)S(1)}, u32[]{:S(2)}, u32[]{:S(2)}) collective-permute-start(f32[48,2048]{1,0:T(8,128)S(1)} %collective-permute-done.4.refs_0_), channel_id=1, source_target_pairs={{0,16},{1,17},{2,18},{3,19},{4,20},{5,21},{6,22},{7,23},{8,24},{9,... | collective-permute-start | bytes 1179656 | tf_op jit(solution)/shard_map/ppermute | solution.py:145
  54.4 19.7 %collective-permute-start.9 = (f32[48,2048]{1,0:T(8,128)S(1)}, f32[48,2048]{1,0:T(8,128)S(1)}, u32[]{:S(2)}, u32[]{:S(2)}) collective-permute-start(f32[48,2048]{1,0:T(8,128)S(1)} %collective-permute-done.5.refs_2_), channel_id=1, source_target_pairs={{0,16},{1,17},{2,18},{3,19},{4,20},{5,21},{6,22},{7,23},{8,24},{9,... | collective-permute-start | bytes 1179656 | tf_op jit(solution)/shard_map/ppermute | solution.py:145
  74.0 2.9 %collective-permute-start.14 = (f32[48,2048]{1,0:T(8,128)S(1)}, f32[48,2048]{1,0:T(8,128)S(1)}, u32[]{:S(2)}, u32[]{:S(2)}) collective-permute-start(f32[48,2048]{1,0:T(8,128)S(1)} %collective-permute-done.9.refs_2_), channel_id=1, source_target_pairs={{0,8},{1,9},{2,10},{3,11},{4,12},{5,13},{6,14},{7,15},{8,0},{9,1},... | collective-permute-start | bytes 1179656 | tf_op jit(solution)/shard_map/ppermute | solution.py:145
  74.0 2.9 %collective-permute-start.15 = (f32[48,2048]{1,0:T(8,128)S(1)}, f32[48,2048]{1,0:T(8,128)S(1)}, u32[]{:S(2)}, u32[]{:S(2)}) collective-permute-start(f32[48,2048]{1,0:T(8,128)S(1)} %collective-permute-done.8.refs_0_), channel_id=1, source_target_pairs={{0,8},{1,9},{2,10},{3,11},{4,12},{5,13},{6,14},{7,15},{8,0},{9,1},... | collective-permute-start | bytes 1179656 | tf_op jit(solution)/shard_map/ppermute | solution.py:145
  74.6 11.3 %collective-permute-start.3 = (f32[48,2048]{1,0:T(8,128)S(1)}, f32[48,2048]{1,0:T(8,128)S(1)}, u32[]{:S(2)}, u32[]{:S(2)}) collective-permute-start(f32[48,2048]{1,0:T(8,128)S(1)} %shard_map.28.refs_0_), channel_id=1, source_target_pairs={{0,16},{1,17},{2,18},{3,19},{4,20},{5,21},{6,22},{7,23},{8,24},{9,... | collective-permute-start | bytes 1179656 | tf_op jit(solution)/shard_map/ppermute | solution.py:145
  75.1 13.9 %collective-permute-start.22 = (f32[96,1536]{1,0:T(8,128)S(1)}, f32[96,1536]{1,0:T(8,128)S(1)}, u32[]{:S(2)}, u32[]{:S(2)}) collective-permute-start(f32[96,1536]{1,0:T(8,128)S(1)} %shard_map.32), channel_id=1, source_target_pairs={{0,32},{1,33},{2,34},{3,35},{4,36},{5,37},{6,38},{7,39},{8,104},{9... | collective-permute-start | bytes 1769480 | tf_op jit(solution)/shard_map/ppermute | solution.py:145
  75.4 19.5 %collective-permute-start.19 = (f32[96,1536]{1,0:T(8,128)S(1)}, f32[96,1536]{1,0:T(8,128)S(1)}, u32[]{:S(2)}, u32[]{:S(2)}) collective-permute-start(f32[96,1536]{1,0:T(8,128)S(1)} %shard_map.34), channel_id=1, source_target_pairs={{0,32},{1,33},{2,34},{3,35},{4,36},{5,37},{6,38},{7,39},{8,104},{9... | collective-permute-start | bytes 1769480 | tf_op jit(solution)/shard_map/ppermute | solution.py:145
  85.9 10.5 %collective-permute-start.16 = (f32[48,2048]{1,0:T(8,128)S(1)}, f32[48,2048]{1,0:T(8,128)S(1)}, u32[]{:S(2)}, u32[]{:S(2)}) collective-permute-start(f32[48,2048]{1,0:T(8,128)S(1)} %shard_map.28.refs_0_), channel_id=1, source_target_pairs={{0,8},{1,9},{2,10},{3,11},{4,12},{5,13},{6,14},{7,15},{8,0},{9,1},... | collective-permute-start | bytes 1179656 | tf_op jit(solution)/shard_map/ppermute | solution.py:145
  85.9 11.7 %collective-permute-start.17 = (f32[48,2048]{1,0:T(8,128)S(1)}, f32[48,2048]{1,0:T(8,128)S(1)}, u32[]{:S(2)}, u32[]{:S(2)}) collective-permute-start(f32[48,2048]{1,0:T(8,128)S(1)} %collective-permute-done.3.refs_2_), channel_id=1, source_target_pairs={{0,8},{1,9},{2,10},{3,11},{4,12},{5,13},{6,14},{7,15},{8,0},{9,1},... | collective-permute-start | bytes 1179656 | tf_op jit(solution)/shard_map/ppermute | solution.py:145
  86.4 16.3 %collective-permute-start.21 = (f32[96,1536]{1,0:T(8,128)S(1)}, f32[96,1536]{1,0:T(8,128)S(1)}, u32[]{:S(2)}, u32[]{:S(2)}) collective-permute-start(f32[96,1536]{1,0:T(8,128)S(1)} %get-tuple-element.54), channel_id=1, source_target_pairs={{0,96},{1,97},{2,98},{3,99},{4,100},{5,101},{6,102},{7,103},{8,40}... | collective-permute-start | bytes 1769480 | tf_op jit(solution)/shard_map/ppermute | solution.py:145
  89.1 18.4 %collective-permute-start.23 = (f32[96,1536]{1,0:T(8,128)S(1)}, f32[96,1536]{1,0:T(8,128)S(1)}, u32[]{:S(2)}, u32[]{:S(2)}) collective-permute-start(f32[96,1536]{1,0:T(8,128)S(1)} %add.72), channel_id=1, source_target_pairs={{0,32},{1,33},{2,34},{3,35},{4,36},{5,37},{6,38},{7,39},{8,104},{9... | collective-permute-start | bytes 1769480 | tf_op jit(solution)/shard_map/ppermute | solution.py:145
  94.9 20.5 %collective-permute-start.18 = (f32[96,1536]{1,0:T(8,128)S(1)}, f32[96,1536]{1,0:T(8,128)S(1)}, u32[]{:S(2)}, u32[]{:S(2)}) collective-permute-start(f32[96,1536]{1,0:T(8,128)S(1)} %get-tuple-element.52), channel_id=1, source_target_pairs={{0,96},{1,97},{2,98},{3,99},{4,100},{5,101},{6,102},{7,103},{8,40}... | collective-permute-start | bytes 1769480 | tf_op jit(solution)/shard_map/ppermute | solution.py:145
  96.4 21.4 %collective-permute-start.20 = (f32[96,1536]{1,0:T(8,128)S(1)}, f32[96,1536]{1,0:T(8,128)S(1)}, u32[]{:S(2)}, u32[]{:S(2)}) collective-permute-start(f32[96,1536]{1,0:T(8,128)S(1)} %add.71), channel_id=1, source_target_pairs={{0,32},{1,33},{2,34},{3,35},{4,36},{5,37},{6,38},{7,39},{8,104},{9... | collective-permute-start | bytes 1769480 | tf_op jit(solution)/shard_map/ppermute | solution.py:145
